TPU v7x, 32 devices: a whole 2x2x4 slice. The times are simulated.
32 devices in a mesh: group: 2 (over y), expert: 4 (over x, core), tensor: 4 (over z).
Axes of the slice: x: 2, y: 2, z: 4, core: 2. Of those that a mesh axis runs over, the one named last changes fastest.
Arguments:
- tokens: bfloat16 [512, 4096], P(('group', 'expert'), 'tensor'), parts along dimension 0, may hold values from -6 to 6
- w_gate: bfloat16 [8, 4096, 1536], P('expert', 'tensor'), may hold values from -0.125 to 0.125
- w_up: bfloat16 [8, 4096, 1536], P('expert', 'tensor'), may hold values from -0.125 to 0.125
- w_down: bfloat16 [8, 1536, 4096], P('expert', None, 'tensor'), may hold values from -0.15625 to 0.15625
- expert_ids: int32 [512, 8], P(('group', 'expert')), parts along dimension 0, may hold values from 0 to 7, as said below
- route_weights: float32 [512, 8], P(('group', 'expert')), parts along dimension 0, may hold values from 0.05 to 0.5
Outputs:
- mixed_out: bfloat16 [512, 4096], P(('group', 'expert'), 'tensor'), parts along dimension 0
There are 2 independent parts, one for each index of `group`. A program takes and returns all parts, laid end to end along the dimension named above; an argument that names none is the same for every part. Nothing has to cross between parts.
Inputs may be any that keep to these rules, and one draw needn't show every extreme that they name: `expert_ids`: each row names 8 different experts. In each aligned block of 64 rows no expert is named by more than 64 rows, and one expert, the same in every block of a part, is named by exactly 64 rows of every block.
All inputs are finite; a program needn't handle non-finite values.
Results may differ from a plain program's by a relative error of at most 0.0057.
Values may be sent and summed in bfloat16 or wider, within the bound.
No kernel may reach another device: no remote copies, remote signals or barrier semaphores. Data moves between devices by JAX's collectives and lax.ppermute only.
A program may use at most 128 MiB of HBM per device.

v0:
```python
import jax
import jax.numpy as jnp
from jax import lax
from jax.sharding import PartitionSpec as P


def slot_numbers(flat_ids, experts_all):
    labels = jnp.arange(experts_all, dtype=jnp.int32)
    onehot = (flat_ids[:, None] == labels[None, :]).astype(jnp.int32)
    before = jnp.cumsum(onehot, axis=0) - onehot
    return jnp.sum(before * onehot, axis=1)


def per_device(tokens, w_gate, w_up, w_down, expert_ids, route_weights):
    n_expert = lax.axis_size("expert")
    held_experts = w_gate.shape[0]
    experts_all = held_experts * n_expert
    tok_rows = tokens.shape[0]
    col_share = tokens.shape[1]
    per_token = expert_ids.shape[1]
    capacity = min(tok_rows, 2 * tok_rows * per_token // experts_all)
    flat_ids = expert_ids.reshape(tok_rows * per_token)
    position = flat_ids * capacity + slot_numbers(flat_ids, experts_all)
    owners = jnp.arange(tok_rows * per_token, dtype=jnp.int32) // per_token
    source = jnp.full((experts_all * capacity,), -1, jnp.int32).at[position].set(owners)
    filled = (source >= 0)[:, None]
    picked_rows = jnp.where(filled, tokens[jnp.maximum(source, 0)], jnp.zeros((), tokens.dtype))
    outgoing = picked_rows.reshape(n_expert, held_experts, capacity, col_share)
    received = lax.all_to_all(outgoing, "expert", split_axis=0, concat_axis=0, tiled=True)
    gate_part = jnp.einsum("sjnd,jdf->sjnf", received, w_gate, preferred_element_type=jnp.float32)
    up_part = jnp.einsum("sjnd,jdf->sjnf", received, w_up, preferred_element_type=jnp.float32)
    gate_share = lax.psum_scatter(gate_part, "tensor", scatter_dimension=3, tiled=True)
    up_share = lax.psum_scatter(up_part, "tensor", scatter_dimension=3, tiled=True)
    hidden_share = (jax.nn.silu(gate_share) * up_share).astype(jnp.bfloat16)
    hidden = lax.all_gather(hidden_share, "tensor", axis=3, tiled=True)
    result = jnp.einsum("sjnf,jfd->sjnd", hidden, w_down, preferred_element_type=jnp.float32)
    returned = result.astype(jnp.bfloat16)
    combined = lax.all_to_all(returned, "expert", split_axis=0, concat_axis=0, tiled=True).reshape(
        experts_all * capacity, col_share
    )
    picked = combined[position].reshape(tok_rows, per_token, col_share).astype(jnp.float32)
    mixed_out = jnp.sum(picked * route_weights[:, :, None], axis=1)
    return mixed_out.astype(jnp.bfloat16)


def solution(mesh):
    in_specs = (
        P(("group", "expert"), "tensor"),
        P("expert", "tensor", None),
        P("expert", "tensor", None),
        P("expert", None, "tensor"),
        P(("group", "expert"), None),
        P(("group", "expert"), None),
    )
    out_specs = P(("group", "expert"), "tensor")
    return jax.shard_map(
        per_device, mesh=mesh, in_specs=in_specs, out_specs=out_specs, check_vma=False
    )
```

profile of v0, /device:TPU:0, one launch (start us, length us, event | category | flops | bytes accessed | tf_op | source)
XLA Modules:
  0.0 236.0 jit_solution(6427868677075579159)
XLA Ops:
  6.5 0.0 copy-start
  6.5 0.0 reduce-scatter.3.cloned.1.call-start
  6.5 0.8 copy.16
  7.3 0.1 eq.29
  7.4 0.1 eq.25
  7.5 0.7 broadcast_multiply_fusion
  8.2 1.1 reduce-window.6
  9.4 0.2 slice_reduce_fusion
  9.6 0.1 copy.15
  9.7 0.1 mul.32
  9.8 0.1 fusion.22
  9.9 2.4 %scatter_custom_fusion = s32[512]{0:T(512)S(1)} fusion(s32[512]{0:T(512)S(1)} %bitcast.47, s32[512]{0:T(512)S(1)} %add_select_fusion, s32[]{:T(128)} %constant.27.clone.1), kind=kCustom, calls=%fused_computation.39 | custom fusion | bytes 2052 | tf_op jit(solution)/shard_map/scatter | solution.py:25
  12.4 0.1 broadcast_in_dim.26
  12.5 0.0 copy-done
  12.5 2.1 gather_fusion
  14.5 0.1 broadcast_select_fusion
  14.7 18.5 %all_to_all.10 = bf16[4,2,64,1024]{3,2,1,0:T(8,128)(2,1)S(1)} all-to-all(bf16[4,2,64,1024]{3,2,1,0:T(8,128)(2,1)S(1)} %broadcast_select_fusion), channel_id=1, replica_groups=mesh['group'=2,'expert'=4,'tensor'=4] {'expert'}, dimensions={0} | all-to-all | bytes 2097152 | tf_op jit(solution)/shard_map/all_to_all | solution.py:29
  33.2 6.3 %fusion.6 = f32[4,2,64,1536]{3,2,0,1:T(8,128)} fusion(bf16[2,1024,1536]{2,1,0:T(8,128)(2,1)} %param.7, bf16[4,2,64,1024]{3,2,1,0:T(8,128)(2,1)S(1)} %all_to_all.10), kind=kOutput, calls=%fused_computation.9 | convolution fusion | flops 1610612736 | bytes 10485760 | tf_op jit(solution)/shard_map/sjnd,jdf->sjnf/dot_general | solution.py:30
  39.4 0.0 reduce-scatter.3.cloned.1.call-update
  39.5 0.0 reduce-scatter.5.cloned.1.call-start
  39.5 6.3 %fusion.9 = f32[4,2,64,1536]{3,2,0,1:T(8,128)} fusion(bf16[2,1024,1536]{2,1,0:T(8,128)(2,1)} %param.8, bf16[4,2,64,1024]{3,2,1,0:T(8,128)(2,1)S(1)} %all_to_all.10), kind=kOutput, calls=%fused_computation.10 | convolution fusion | flops 1610612736 | bytes 10485760 | tf_op jit(solution)/shard_map/sjnd,jdf->sjnf/dot_general | solution.py:31
  45.8 0.0 reduce-scatter.5.cloned.1.call-update
  45.8 0.0 all-gather.2.cloned.1.call-start
  45.9 54.4 %reduce-scatter.3.cloned.1.call-done = f32[4,2,64,384]{3,2,0,1:T(8,128)} async-done(((f32[4,2,64,1536]{3,2,0,1:T(8,128)}), f32[4,2,64,384]{3,2,0,1:T(8,128)}) %reduce-scatter.3.cloned.1.call-update) | async-done | bytes 786448 | tf_op jit(solution)/shard_map/reduce_scatter | solution.py:32
  100.3 62.6 %reduce-scatter.5.cloned.1.call-done = f32[4,2,64,384]{3,2,0,1:T(8,128)} async-done(((f32[4,2,64,1536]{3,2,0,1:T(8,128)}), f32[4,2,64,384]{3,2,0,1:T(8,128)}) %reduce-scatter.5.cloned.1.call-update) | async-done | bytes 786448 | tf_op jit(solution)/shard_map/reduce_scatter | solution.py:33
  163.0 2.3 multiply_convert_fusion
  165.3 0.0 all-gather.2.cloned.1.call-update
  165.3 0.0 copy-start.1
  165.3 36.7 %all-gather.2.cloned.1.call-done = bf16[4,2,64,1536]{3,2,0,1:T(8,128)(2,1)} async-done(((bf16[4,2,64,384]{3,2,0,1:T(8,128)(2,1)}), bf16[4,2,64,1536]{3,2,0,1:T(8,128)(2,1)}) %all-gather.2.cloned.1.call-update) | async-done | bytes 1572880 | tf_op jit(solution)/shard_map/all_gather | solution.py:35
  202.0 5.1 %fusion.16 = bf16[4,2,64,1024]{3,2,0,1:T(8,128)(2,1)S(1)} fusion(bf16[4,2,64,1536]{3,2,0,1:T(8,128)(2,1)} %all-gather.2.cloned.1.call-done, bf16[2,1536,1024]{2,1,0:T(8,128)(2,1)} %param.9), kind=kOutput, calls=%fused_computation.14 | convolution fusion | flops 1611137024 | bytes 8912896 | tf_op jit(solution)/shard_map/sjnf,jfd->sjnd/dot_general | solution.py:36
  207.1 1.1 copy.20
  208.1 3.5 %all-to-all-start.1 = ((bf16[4,2,64,1024]{3,2,1,0:T(8,128)(2,1)}), bf16[4,2,64,1024]{3,2,1,0:T(8,128)(2,1)S(1)}, u32[]{:S(2)}, u32[]{:S(2)}) async-start(bf16[4,2,64,1024]{3,2,1,0:T(8,128)(2,1)} %copy.20), calls=%async_computation.3 | async-start | bytes 2097152 | tf_op jit(solution)/shard_map/all_to_all | solution.py:38
  211.7 0.0 copy-done.1
  211.7 0.1 copy.21
  211.8 14.3 %all-to-all-done.1 = bf16[4,2,64,1024]{3,2,1,0:T(8,128)(2,1)S(1)} async-done(((bf16[4,2,64,1024]{3,2,1,0:T(8,128)(2,1)}), bf16[4,2,64,1024]{3,2,1,0:T(8,128)(2,1)S(1)}, u32[]{:S(2)}, u32[]{:S(2)}) %all-to-all-start.1) | async-done | bytes 1048608 | tf_op jit(solution)/shard_map/all_to_all | solution.py:38
  226.1 2.0 gather_fusion.1
  228.1 1.4 fusion.12
  (9 shorter events, 0.1 us)
Async XLA Ops:
  6.5 6.0 %copy-start = (bf16[64,1024]{1,0:T(8,128)(2,1)S(1)}, bf16[64,1024]{1,0:T(8,128)(2,1)}, u32[]{:S(2)}) copy-start(bf16[64,1024]{1,0:T(8,128)(2,1)} %param.6) | copy-start | bytes 393220
  6.5 93.8 %reduce-scatter.3.cloned.1.call-start = ((), (), s32[]{:S(2)}) async-start(), calls=%async_computation.4 | async-start | bytes 3932160 | tf_op jit(solution)/shard_map/reduce_scatter | solution.py:32
  39.5 123.5 %reduce-scatter.5.cloned.1.call-start = ((), (), s32[]{:S(2)}) async-start(), calls=%async_computation.5 | async-start | bytes 3932160 | tf_op jit(solution)/shard_map/reduce_scatter | solution.py:33
  45.8 156.2 %all-gather.2.cloned.1.call-start = ((), (), s32[]{:S(2)}) async-start(), calls=%async_computation.6 | async-start | bytes 1966080 | tf_op jit(solution)/shard_map/all_gather | solution.py:35
  165.3 46.3 %copy-start.1 = (f32[64,8]{0,1:T(8,128)S(1)}, f32[64,8]{0,1:T(8,128)}, u32[]{:S(2)}) copy-start(f32[64,8]{0,1:T(8,128)} %param.11) | copy-start | bytes 6148
  208.1 17.9 %all-to-all-start.1 = ((bf16[4,2,64,1024]{3,2,1,0:T(8,128)(2,1)}), bf16[4,2,64,1024]{3,2,1,0:T(8,128)(2,1)S(1)}, u32[]{:S(2)}, u32[]{:S(2)}) async-start(bf16[4,2,64,1024]{3,2,1,0:T(8,128)(2,1)} %copy.20), calls=%async_computation.3 | async-start | bytes 2097152 | tf_op jit(solution)/shard_map/all_to_all | solution.py:38
Sparse Core Ops, SparseCore 0:
  39.6 60.6 reduce-scatter.2
  102.6 60.3 reduce-scatter.4
  165.4 36.5 all-gather.1
where the time goes:
time: 236 us
  waiting for transfers between devices  168 us (71%)
  blocking collectives  18.5 us (8%)
  matrix products  17.6 us (7%)
  between operations  13.2 us (6%)
  local copies, waits for them, and re-layouts  9.18 us (4%)
  other arithmetic  5.83 us (2%)
  starting transfers between devices  3.6 us (2%)
    reduce_scatter x1, waiting for transfers between devices, per_device(): lax.psum_scatter(up_part, 'tensor', scatter_dimension=3, tiled=True)  62.6 us
    reduce_scatter x1, waiting for transfers between devices, per_device(): lax.psum_scatter(gate_part, 'tensor', scatter_dimension=3, tiled=True)  54.4 us
    all_gather x1, waiting for transfers between devices, per_device(): hidden = lax.all_gather(hidden_share, 'tensor', axis=3, tiled=True)  36.7 us
    all_to_all x1, blocking collectives, per_device(): lax.all_to_all(outgoing, 'expert', split_axis=0, concat_axis=0, tiled=True)  18.5 us
    all_to_all x1, waiting for transfers between devices, per_device(): lax.all_to_all(returned, 'expert', split_axis=0, concat_axis=0, tiled=True)  14.3 us
    dot_general x1, matrix products, per_device(): jnp.einsum('sjnd,jdf->sjnf', received, w_up, preferred_element_type=jnp.f...  6.3 us
    dot_general x1, matrix products, per_device(): jnp.einsum('sjnd,jdf->sjnf', received, w_gate, preferred_element_type=jnp...  6.27 us
    dot_general x1, matrix products, per_device(): jnp.einsum('sjnf,jfd->sjnd', hidden, w_down, preferred_element_type=jnp.f...  5.06 us
  transfers between devices with their start and end apart: 4, of which 4 were waited for; matrix products, arithmetic and copies ran while one was open for 3% of the time, Pallas kernels for 0%

commit v1 on v0

v1 whole, which is shorter than its diff:
```python
import jax
import jax.numpy as jnp
from jax import lax
from jax.sharding import PartitionSpec as P

CHUNKS = 4


def reduce_to_ends_and_share(gate, up, chunks):
    n = lax.axis_size("tensor")
    place = lax.axis_index("tensor")
    wire = jnp.bfloat16 if n <= 4 else jnp.float32
    experts, rows, width = gate.shape
    half = width // 2
    rb = experts * rows // chunks
    gate = gate.reshape(chunks, rb, width)
    up = up.reshape(chunks, rb, width)

    class Line:
        def __init__(self, forward):
            self.pos = place if forward else n - 1 - place
            self.cols = slice(half, width) if forward else slice(0, half)
            self.dev = (lambda p: p) if forward else (lambda p: n - 1 - p)
            self.recv = None
            self.back = None
            self.out = jnp.zeros((chunks + 1, rb, half), jnp.bfloat16)

        def own(self, k):
            g = lax.dynamic_index_in_dim(gate[:, :, self.cols], k, 0, keepdims=False)
            u = lax.dynamic_index_in_dim(up[:, :, self.cols], k, 0, keepdims=False)
            return g, u

        def send(self, t):
            if t > chunks + n - 3:
                return
            g, u = self.own(jnp.clip(t - self.pos, 0, chunks - 1))
            if self.recv is not None:
                g = g + self.recv[0].astype(jnp.float32)
                u = u + self.recv[1].astype(jnp.float32)
            pairs = [(self.dev(p), self.dev(p + 1)) for p in range(n - 1) if 0 <= t - p < chunks]
            self.recv = lax.ppermute(jnp.stack([g.astype(wire), u.astype(wire)]), "tensor", pairs)

        def finish(self, m):
            if m >= chunks:
                return None
            g = gate[m][:, self.cols] + self.recv[0].astype(jnp.float32)
            u = up[m][:, self.cols] + self.recv[1].astype(jnp.float32)
            return (jax.nn.silu(g) * u).astype(jnp.bfloat16)

        def share(self, t, mine):
            last = self.pos == n - 1
            if mine is None:
                outgoing = self.back
            else:
                self.out = self.store(jnp.where(last, t, chunks), mine)
                outgoing = mine if self.back is None else jnp.where(last, mine, self.back)
            hops = [h for h in range(n - 1) if 0 <= t - h < chunks]
            pairs = [(self.dev(n - 1 - h), self.dev(n - 2 - h)) for h in hops]
            self.back = lax.ppermute(outgoing, "tensor", pairs)
            k = t - (n - 2 - self.pos)
            ok = (k >= 0) & (k < chunks) & (self.pos < n - 1)
            self.out = self.store(jnp.where(ok, k, chunks), self.back)

        def store(self, k, block):
            return lax.dynamic_update_index_in_dim(self.out, block, k, 0)

    lines = (Line(False), Line(True))
    for t in range(chunks + 2 * n - 3):
        m = t - (n - 1)
        mine = [line.finish(m) if m >= 0 else None for line in lines]
        for line in lines:
            line.send(t)
        if m >= 0:
            for line, block in zip(lines, mine):
                line.share(m, block)
    return [line.out[:chunks].reshape(experts, rows, half) for line in lines]


def per_device(tokens, w_gate, w_up, w_down, expert_ids, route_weights):
    n_expert = lax.axis_size("expert")
    held = w_gate.shape[0]
    tok_rows, col_share = tokens.shape
    labels = jnp.arange(held * n_expert, dtype=jnp.int32)
    chosen = expert_ids[:, :, None] == labels[None, None, :]
    dense = jnp.sum(jnp.where(chosen, route_weights[:, :, None], 0.0), axis=1)
    rows_in = lax.all_gather(tokens, "expert", axis=0, tiled=True)
    dense = dense.reshape(tok_rows, n_expert, held).transpose(1, 2, 0)
    weights = lax.all_to_all(dense, "expert", split_axis=0, concat_axis=0, tiled=True)
    weights = weights.transpose(1, 0, 2).reshape(held, n_expert * tok_rows)
    gate = jnp.einsum("td,edf->etf", rows_in, w_gate, preferred_element_type=jnp.float32)
    up = jnp.einsum("td,edf->etf", rows_in, w_up, preferred_element_type=jnp.float32)
    low, high = reduce_to_ends_and_share(gate, up, CHUNKS)
    hidden = jnp.concatenate([low, high], axis=2)
    result = jnp.einsum("etf,efd->etd", hidden, w_down, preferred_element_type=jnp.float32)
    partial = jnp.sum(result * weights[:, :, None], axis=0).astype(jnp.bfloat16)
    partial = partial.reshape(n_expert, tok_rows, col_share)
    pieces = lax.all_to_all(partial, "expert", split_axis=0, concat_axis=0, tiled=True)
    return jnp.sum(pieces.astype(jnp.float32), axis=0).astype(jnp.bfloat16)


def solution(mesh):
    in_specs = (
        P(("group", "expert"), "tensor"),
        P("expert", "tensor", None),
        P("expert", "tensor", None),
        P("expert", None, "tensor"),
        P(("group", "expert"), None),
        P(("group", "expert"), None),
    )
    out_specs = P(("group", "expert"), "tensor")
    return jax.shard_map(
        per_device, mesh=mesh, in_specs=in_specs, out_specs=out_specs, check_vma=False
    )
```

time: 236 us -> 167 us (0.71)
  waiting for transfers between devices: 168 us -> 58.9 us
  starting transfers between devices: 3.6 us -> 51.5 us
  between operations: 13.2 us -> 0.76 us
  matrix products: 17.6 us -> 11.1 us
  other arithmetic: 5.83 us -> 12.3 us
  local copies, waits for them, and re-layouts: 9.18 us -> 11.6 us
    reduce_scatter x2 -> x0, waiting for transfers between devices: 117 us -> none  [the longest x1 62.6 us: per_device(): lax.psum_scatter(up_part, 'tensor', scatter_dimension=3, tiled=True)]
    ppermute x0 -> x24, waiting for transfers between devices: none -> 58.9 us  [the longest x12 29.5 us: share(): self.back = lax.ppermute(outgoing, 'tensor', pairs)]
    ppermute x0 -> x24, starting transfers between devices: none -> 48.3 us  [the longest x12 28.2 us: send(): lax.ppermute(jnp.stack([g.astype(wire), u.astype(wire)]), 'tensor', pairs)]
    all_gather x1 -> x0, waiting for transfers between devices: 36.7 us -> none  [per_device(): hidden = lax.all_gather(hidden_share, 'tensor', axis=3, tiled=True)]
    all_to_all x1, waiting for transfers between devices: 14.3 us -> 0.01 us  [per_device(): lax.all_to_all(dense, 'expert', split_axis=0, concat_axis=0, tiled=True)]
    all_gather x0 -> x1, blocking collectives: none -> 8.97 us  [per_device(): rows_in = lax.all_gather(tokens, 'expert', axis=0, tiled=True)]
    all_to_all x1, blocking collectives: 18.5 us -> 11.2 us  [per_device(): lax.all_to_all(partial, 'expert', split_axis=0, concat_axis=0, tiled=True)]
    dot_general x3, matrix products: 17.6 us -> 11.1 us  [the longest x1 4.72 us: per_device(): jnp.einsum('td,edf->etf', rows_in, w_gate, preferred_element_type=jnp.flo...]
  transfers between devices with their start and end apart: 4 -> 25, of which waited for: 4 -> 14; matrix products, arithmetic and copies ran while one was open for 3% -> 10% of each run, Pallas kernels for 0% -> 0%
where the time goes in v1:
time: 167 us; the launch traced here: 166 us
  waiting for transfers between devices  58.9 us (35%)
  starting transfers between devices  51.5 us (31%)
  blocking collectives  20.2 us (12%)
  other arithmetic  12.3 us (7%)
  local copies, waits for them, and re-layouts  11.6 us (7%)
  matrix products  11.1 us (7%)
    ppermute x12, waiting for transfers between devices, share(): self.back = lax.ppermute(outgoing, 'tensor', pairs)  29.5 us
    ppermute x12, waiting for transfers between devices, send(): lax.ppermute(jnp.stack([g.astype(wire), u.astype(wire)]), 'tensor', pairs)  29.4 us
    ppermute x12, starting transfers between devices, send(): lax.ppermute(jnp.stack([g.astype(wire), u.astype(wire)]), 'tensor', pairs)  28.2 us
    ppermute x12, starting transfers between devices, share(): self.back = lax.ppermute(outgoing, 'tensor', pairs)  20.1 us
    all_to_all x1, blocking collectives, per_device(): lax.all_to_all(partial, 'expert', split_axis=0, concat_axis=0, tiled=True)  11.2 us
    all_gather x1, blocking collectives, per_device(): rows_in = lax.all_gather(tokens, 'expert', axis=0, tiled=True)  8.97 us
    convert_element_type x10, other arithmetic, send(): g.astype(wire)  6.02 us
    dot_general x1, matrix products, per_device(): jnp.einsum('td,edf->etf', rows_in, w_gate, preferred_element_type=jnp.flo...  4.72 us
  transfers between devices with their start and end apart: 25, of which 14 were waited for; matrix products, arithmetic and copies ran while one was open for 10% of the time, Pallas kernels for 0%

profile of v1, /device:TPU:0, one launch (start us, length us, event | category | flops | bytes accessed | tf_op | source)
XLA Modules:
  0.0 166.5 jit_solution(3197572910256677994)
XLA Ops:
  0.0 9.0 %all_gather.3 = bf16[256,1024]{1,0:T(8,128)(2,1)S(1)} all-gather(bf16[64,1024]{1,0:T(8,128)(2,1)} %param.6), channel_id=1, replica_groups=mesh['group'=2,'expert'=4,'tensor'=4] {'expert'}, dimensions={0}, use_global_device_ids=true | all-gather | bytes 655360 | tf_op jit(solution)/shard_map/all_gather | solution.py:86
  9.0 4.7 %fusion.3 = f32[2,1536,256]{1,2,0:T(8,128)S(1)} fusion(bf16[2,1024,1536]{2,1,0:T(8,128)(2,1)} %param.7, bf16[256,1024]{1,0:T(8,128)(2,1)S(1)} %all_gather.3), kind=kOutput, calls=%fused_computation.12 | convolution fusion | flops 1610612736 | bytes 9961472 | tf_op jit(solution)/shard_map/td,edf->etf/dot_general | solution.py:90
  13.7 1.8 %fusion.5 = f32[2,1536,256]{1,2,0:T(8,128)S(1)} fusion(bf16[2,1024,1536]{2,1,0:T(8,128)(2,1)S(1)} %bitcast.202, bf16[256,1024]{1,0:T(8,128)(2,1)S(1)} %all_gather.3), kind=kOutput, calls=%fused_computation.14 | convolution fusion | flops 1610612736 | bytes 9961472 | tf_op jit(solution)/shard_map/td,edf->etf/dot_general | solution.py:91
  15.5 2.2 %fusion.57 = (f32[4,128,768]{2,1,0:T(8,128)}, f32[4,128,768]{2,1,0:T(8,128)}) fusion(f32[4,128,1536]{2,1,0:T(8,128)S(1)} %bitcast.199), kind=kLoop, calls=%fused_computation.142 | loop fusion | bytes 6291456 | tf_op jit(solution)/shard_map/slice | solution.py:30
  17.7 0.4 copy-done
  18.2 2.0 %fusion.56 = (f32[4,128,768]{2,1,0:T(8,128)}, f32[4,128,768]{2,1,0:T(8,128)}) fusion(f32[4,128,1536]{2,1,0:T(8,128)S(1)} %bitcast.197), kind=kLoop, calls=%fused_computation.141 | loop fusion | bytes 6291456 | tf_op jit(solution)/shard_map/slice | solution.py:29
  20.2 1.2 dynamic-slice_convert_fusion
  21.3 0.8 pad_maximum_fusion.6
  22.1 4.3 %collective-permute-start.12 = (bf16[2,128,768]{2,1,0:T(8,128)(2,1)}, bf16[2,128,768]{2,1,0:T(8,128)(2,1)}, u32[]{:S(2)}, u32[]{:S(2)}) collective-permute-start(bf16[2,128,768]{2,1,0:T(8,128)(2,1)} %pad_maximum_fusion.6), channel_id=1, source_target_pairs={{0,1},{4,5},{8,9},{12,13},{16,17},{20,21},{24,25},{28,29}} | collective-permute-start | bytes 1179656 | tf_op jit(solution)/shard_map/ppermute | solution.py:41
  26.4 1.2 dynamic-slice_convert_fusion.2
  27.6 1.4 collective-permute-start
  29.1 5.7 %collective-permute-done.12 = bf16[2,128,768]{2,1,0:T(8,128)(2,1)} collective-permute-done((bf16[2,128,768]{2,1,0:T(8,128)(2,1)}, bf16[2,128,768]{2,1,0:T(8,128)(2,1)}, u32[]{:S(2)}, u32[]{:S(2)}) %collective-permute-start.12) | collective-permute-done | bytes 393248 | tf_op jit(solution)/shard_map/ppermute | solution.py:41
  34.8 1.4 add_convert_fusion.3
  36.2 0.8 pad_maximum_fusion.7
  37.0 5.2 %collective-permute-start.13 = (bf16[2,128,768]{2,1,0:T(8,128)(2,1)}, bf16[2,128,768]{2,1,0:T(8,128)(2,1)}, u32[]{:S(2)}, u32[]{:S(2)}) collective-permute-start(bf16[2,128,768]{2,1,0:T(8,128)(2,1)} %pad_maximum_fusion.7), channel_id=1, source_target_pairs={{0,1},{1,2},{4,5},{5,6},{8,9},{9,10},{12,13},{13,14},{16,17},{17,1... | collective-permute-start | bytes 1179656 | tf_op jit(solution)/shard_map/ppermute | solution.py:41
  42.1 0.7 reshape.75
  42.8 3.2 %all-to-all-start = ((f32[4,1,128]{2,1,0:T(1,128)}), f32[4,1,128]{2,1,0:T(1,128)S(1)}, u32[]{:S(2)}, u32[]{:S(2)}) async-start(f32[4,1,128]{2,1,0:T(1,128)} %reshape.75), calls=%async_computation | async-start | bytes 4096 | tf_op jit(solution)/shard_map/all_to_all | solution.py:88
  46.0 1.4 add_convert_fusion.7
  47.4 0.8 pad_maximum_fusion.1
  48.2 1.5 collective-permute-start.1
  49.8 1.4 add_convert_fusion.1
  51.1 0.8 pad_maximum_fusion.8
  51.9 4.3 %collective-permute-start.14 = (bf16[2,128,768]{2,1,0:T(8,128)(2,1)}, bf16[2,128,768]{2,1,0:T(8,128)(2,1)S(1)}, u32[]{:S(2)}, u32[]{:S(2)}) collective-permute-start(bf16[2,128,768]{2,1,0:T(8,128)(2,1)} %pad_maximum_fusion.8), channel_id=1, source_target_pairs={{0,1},{1,2},{2,3},{4,5},{5,6},{6,7},{8,9},{9,10},{10,11},{12,13},{... | collective-permute-start | bytes 1179656 | tf_op jit(solution)/shard_map/ppermute | solution.py:41
  56.2 2.7 %slice_bitcast_fusion = (f32[128,1536]{1,0:T(8,128)}, f32[128,1536]{1,0:T(8,128)}, f32[128,1536]{1,0:T(8,128)}, f32[128,1536]{1,0:T(8,128)}, f32[128,1536]{1,0:T...) fusion(f32[4,128,1536]{2,1,0:T(8,128)S(1)} %bitcast.200, f32[4,128,1536]{2,1,0:T(8,128)S(1)} %bitcast.198), kind=kLoop, calls=%fused_computation.4 | loop fusion | bytes 12582912 | tf_op jit(solution)/shard_map/squeeze | solution.py:47
  58.9 0.5 broadcast.15
  59.4 0.7 reduce.1
  60.2 1.5 add_convert_fusion.5
  61.8 1.6 collective-permute-start.2
  63.3 0.3 collective-permute-done.14
  63.9 0.7 collective-permute-start.15
  64.8 4.6 %collective-permute-start.16 = (bf16[2,128,768]{2,1,0:T(8,128)(2,1)S(1)}, bf16[2,128,768]{2,1,0:T(8,128)(2,1)S(1)}, u32[]{:S(2)}, u32[]{:S(2)}) collective-permute-start(bf16[2,128,768]{2,1,0:T(8,128)(2,1)S(1)} %pad_maximum_fusion.9), channel_id=1, source_target_pairs={{0,1},{1,2},{2,3},{4,5},{5,6},{6,7},{8,9},{9,10},{10,11},{12,13},{... | collective-permute-start | bytes 1179656 | tf_op jit(solution)/shard_map/ppermute | solution.py:41
  69.3 4.4 %collective-permute-done.2 = bf16[2,128,768]{2,1,0:T(8,128)(2,1)S(1)} collective-permute-done((bf16[2,128,768]{2,1,0:T(8,128)(2,1)S(1)}, bf16[2,128,768]{2,1,0:T(8,128)(2,1)S(1)}, u32[]{:S(2)}, u32[]{:S(2)}) %collective-permute-start.2) | collective-permute-done | bytes 393248 | tf_op jit(solution)/shard_map/ppermute | solution.py:41
  74.0 3.6 %collective-permute-start.3 = (bf16[128,768]{1,0:T(8,128)(2,1)S(1)}, bf16[128,768]{1,0:T(8,128)(2,1)S(1)}, u32[]{:S(2)}, u32[]{:S(2)}) collective-permute-start(bf16[128,768]{1,0:T(8,128)(2,1)S(1)} %get-tuple-element.12), channel_id=1, source_target_pairs={{0,1},{4,5},{8,9},{12,13},{16,17},{20,21},{24,25},{28,29}} | collective-permute-start | bytes 589832 | tf_op jit(solution)/shard_map/ppermute | solution.py:59
  77.8 1.3 collective-permute-start.4
  79.1 1.6 collective-permute-done.3
  80.9 0.7 collective-permute-start.18
  81.6 7.5 %collective-permute-done.4 = bf16[2,128,768]{2,1,0:T(8,128)(2,1)S(1)} collective-permute-done((bf16[2,128,768]{2,1,0:T(8,128)(2,1)S(1)}, bf16[2,128,768]{2,1,0:T(8,128)(2,1)S(1)}, u32[]{:S(2)}, u32[]{:S(2)}) %collective-permute-start.4) | collective-permute-done | bytes 393248 | tf_op jit(solution)/shard_map/ppermute | solution.py:41
  89.1 0.4 broadcast_select_fusion.5
  89.5 1.6 collective-permute-start.5
  91.1 0.7 collective-permute-start.17
  91.9 1.3 collective-permute-start.6
  93.3 1.0 collective-permute-done.5
  94.5 0.7 collective-permute-start.20
  95.1 7.3 %collective-permute-done.6 = bf16[2,128,768]{2,1,0:T(8,128)(2,1)S(1)} collective-permute-done((bf16[2,128,768]{2,1,0:T(8,128)(2,1)S(1)}, bf16[2,128,768]{2,1,0:T(8,128)(2,1)S(1)}, u32[]{:S(2)}, u32[]{:S(2)}) %collective-permute-start.6) | collective-permute-done | bytes 393248 | tf_op jit(solution)/shard_map/ppermute | solution.py:41
  102.4 0.4 broadcast_select_fusion.4
  102.8 5.6 %collective-permute-start.7 = (bf16[128,768]{1,0:T(8,128)(2,1)S(1)}, bf16[128,768]{1,0:T(8,128)(2,1)S(1)}, u32[]{:S(2)}, u32[]{:S(2)}) collective-permute-start(bf16[128,768]{1,0:T(8,128)(2,1)S(1)} %get-tuple-element.7), channel_id=1, source_target_pairs={{0,1},{1,2},{2,3},{4,5},{5,6},{6,7},{8,9},{9,10},{10,11},{12,13},{... | collective-permute-start | bytes 589832 | tf_op jit(solution)/shard_map/ppermute | solution.py:59
  108.4 1.3 collective-permute-start.19
  109.8 1.4 collective-permute-start.8
  111.6 6.5 %collective-permute-done.19 = bf16[128,768]{1,0:T(8,128)(2,1)S(1)} collective-permute-done((bf16[128,768]{1,0:T(8,128)(2,1)S(1)}, bf16[128,768]{1,0:T(8,128)(2,1)S(1)}, u32[]{:S(2)}, u32[]{:S(2)}) %collective-permute-start.19) | collective-permute-done | bytes 196640 | tf_op jit(solution)/shard_map/ppermute | solution.py:59
  118.1 4.2 %collective-permute-done.8 = bf16[2,128,768]{2,1,0:T(8,128)(2,1)S(1)} collective-permute-done((bf16[2,128,768]{2,1,0:T(8,128)(2,1)S(1)}, bf16[2,128,768]{2,1,0:T(8,128)(2,1)S(1)}, u32[]{:S(2)}, u32[]{:S(2)}) %collective-permute-start.8) | collective-permute-done | bytes 393248 | tf_op jit(solution)/shard_map/ppermute | solution.py:41
  122.3 0.4 broadcast_select_fusion.3
  122.6 1.5 collective-permute-start.9
  124.1 1.3 collective-permute-start.21
  125.5 1.8 %collective-permute-done.9 = bf16[128,768]{1,0:T(8,128)(2,1)S(1)} collective-permute-done((bf16[128,768]{1,0:T(8,128)(2,1)S(1)}, bf16[128,768]{1,0:T(8,128)(2,1)S(1)}, u32[]{:S(2)}, u32[]{:S(2)}) %collective-permute-start.9) | collective-permute-done | bytes 196640 | tf_op jit(solution)/shard_map/ppermute | solution.py:59
  127.3 0.7 collective-permute-start.10
  127.9 4.7 %collective-permute-done.21 = bf16[128,768]{1,0:T(8,128)(2,1)S(1)} collective-permute-done((bf16[128,768]{1,0:T(8,128)(2,1)S(1)}, bf16[128,768]{1,0:T(8,128)(2,1)S(1)}, u32[]{:S(2)}, u32[]{:S(2)}) %collective-permute-start.21) | collective-permute-done | bytes 196640 | tf_op jit(solution)/shard_map/ppermute | solution.py:59
  132.6 1.3 collective-permute-start.22
  134.0 0.7 collective-permute-start.11
  134.6 7.6 %collective-permute-done.22 = bf16[128,768]{1,0:T(8,128)(2,1)S(1)} collective-permute-done((bf16[128,768]{1,0:T(8,128)(2,1)S(1)}, bf16[128,768]{1,0:T(8,128)(2,1)S(1)}, u32[]{:S(2)}, u32[]{:S(2)}) %collective-permute-start.22) | collective-permute-done | bytes 196640 | tf_op jit(solution)/shard_map/ppermute | solution.py:59
  142.2 1.3 collective-permute-start.23
  143.7 6.1 %collective-permute-done.23 = bf16[128,768]{1,0:T(8,128)(2,1)S(1)} collective-permute-done((bf16[128,768]{1,0:T(8,128)(2,1)S(1)}, bf16[128,768]{1,0:T(8,128)(2,1)S(1)}, u32[]{:S(2)}, u32[]{:S(2)}) %collective-permute-start.23) | collective-permute-done | bytes 196640 | tf_op jit(solution)/shard_map/ppermute | solution.py:59
  149.9 4.6 %multiply_reduce_fusion = bf16[256,1024]{1,0:T(8,128)(2,1)S(1)} fusion(bf16[2,1536,1024]{2,1,0:T(8,128)(2,1)} %param.9, bf16[2,256,768]{2,1,0:T(8,128)(2,1)S(1)} %bitcast.204, bf16[2,256,768]{2,1,0:T(8,128)(2,1)S(1)} %bitcast.203, f32[2,256]{1,0:T(2,128)S(1)} %mul.75), kind=kOutput, calls=%fused_computation | convolution fusion | flops 1614544896 | bytes 8390656 | tf_op jit(solution)/shard_map/etf,efd->etd/dot_general | solution.py:94
  154.5 11.2 %all_to_all.10 = bf16[4,64,1024]{2,1,0:T(8,128)(2,1)S(1)} all-to-all(bf16[4,64,1024]{2,1,0:T(8,128)(2,1)S(1)} %bitcast.205), channel_id=1, replica_groups=mesh['group'=2,'expert'=4,'tensor'=4] {'expert'}, dimensions={0} | all-to-all | bytes 1048576 | tf_op jit(solution)/shard_map/all_to_all | solution.py:97
  165.7 0.7 reduce_sum.32
  (90 shorter events, 2.2 us)
Async XLA Ops:
  0.0 13.7 %slice-start = ((s8[6291456]{0:T(1024)(128)(4,1)}), s8[4194304]{0:T(1024)(128)(4,1)S(1)}, s32[]{:S(2)}) async-start(s8[6291456]{0:T(1024)(128)(4,1)} %bitcast.201), calls=%async_computation.2 | async-start | bytes 8388608
  9.0 4.7 %slice-start.1 = ((s8[6291456]{0:T(1024)(128)(4,1)}), s8[2097152]{0:T(1024)(128)(4,1)S(1)}, s32[]{:S(2)}) async-start(s8[6291456]{0:T(1024)(128)(4,1)} %bitcast.201), calls=%async_computation.3 | async-start | bytes 4194304
  15.5 2.6 %copy-start = (f32[2,1536,256]{1,2,0:T(8,128)}, f32[2,1536,256]{1,2,0:T(8,128)S(1)}, u32[]{:S(2)}) copy-start(f32[2,1536,256]{1,2,0:T(8,128)S(1)} %fusion.5) | copy-start | bytes 9437188
  22.1 12.7 %collective-permute-start.12 = (bf16[2,128,768]{2,1,0:T(8,128)(2,1)}, bf16[2,128,768]{2,1,0:T(8,128)(2,1)}, u32[]{:S(2)}, u32[]{:S(2)}) collective-permute-start(bf16[2,128,768]{2,1,0:T(8,128)(2,1)} %pad_maximum_fusion.6), channel_id=1, source_target_pairs={{0,1},{4,5},{8,9},{12,13},{16,17},{20,21},{24,25},{28,29}} | collective-permute-start | bytes 1179656 | tf_op jit(solution)/shard_map/ppermute | solution.py:41
  27.6 14.6 %copy-start.14 = (f32[64,8]{0,1:T(8,128)S(1)}, f32[64,8]{0,1:T(8,128)}, u32[]{:S(2)}) copy-start(f32[64,8]{0,1:T(8,128)} %param.11) | copy-start | bytes 6148
  27.6 14.6 %copy-start.15 = (s32[64,8]{0,1:T(8,128)S(1)}, s32[64,8]{0,1:T(8,128)}, u32[]{:S(2)}) copy-start(s32[64,8]{0,1:T(8,128)} %param.10) | copy-start | bytes 6148
  27.6 18.4 %collective-permute-start = (bf16[2,128,768]{2,1,0:T(8,128)(2,1)S(1)}, bf16[2,128,768]{2,1,0:T(8,128)(2,1)}, u32[]{:S(2)}, u32[]{:S(2)}) collective-permute-start(bf16[2,128,768]{2,1,0:T(8,128)(2,1)S(1)} %pad_maximum_fusion), channel_id=1, source_target_pairs={{3,2},{7,6},{11,10},{15,14},{19,18},{23,22},{27,26},{31,30}} | collective-permute-start | bytes 1179656 | tf_op jit(solution)/shard_map/ppermute | solution.py:41
  37.0 12.8 %collective-permute-start.13 = (bf16[2,128,768]{2,1,0:T(8,128)(2,1)}, bf16[2,128,768]{2,1,0:T(8,128)(2,1)}, u32[]{:S(2)}, u32[]{:S(2)}) collective-permute-start(bf16[2,128,768]{2,1,0:T(8,128)(2,1)} %pad_maximum_fusion.7), channel_id=1, source_target_pairs={{0,1},{1,2},{4,5},{5,6},{8,9},{9,10},{12,13},{13,14},{16,17},{17,1... | collective-permute-start | bytes 1179656 | tf_op jit(solution)/shard_map/ppermute | solution.py:41
  42.8 16.1 %all-to-all-start = ((f32[4,1,128]{2,1,0:T(1,128)}), f32[4,1,128]{2,1,0:T(1,128)S(1)}, u32[]{:S(2)}, u32[]{:S(2)}) async-start(f32[4,1,128]{2,1,0:T(1,128)} %reshape.75), calls=%async_computation | async-start | bytes 4096 | tf_op jit(solution)/shard_map/all_to_all | solution.py:88
  47.4 8.8 %copy-start.1 = (f32[2,1536,256]{1,2,0:T(8,128)S(1)}, f32[2,1536,256]{1,2,0:T(8,128)}, u32[]{:S(2)}) copy-start(f32[2,1536,256]{1,2,0:T(8,128)} %copy-done) | copy-start | bytes 9437188
  48.2 12.0 %collective-permute-start.1 = (bf16[2,128,768]{2,1,0:T(8,128)(2,1)}, bf16[2,128,768]{2,1,0:T(8,128)(2,1)}, u32[]{:S(2)}, u32[]{:S(2)}) collective-permute-start(bf16[2,128,768]{2,1,0:T(8,128)(2,1)} %pad_maximum_fusion.1), channel_id=1, source_target_pairs={{3,2},{2,1},{7,6},{6,5},{11,10},{10,9},{15,14},{14,13},{19,18},{18... | collective-permute-start | bytes 1179656 | tf_op jit(solution)/shard_map/ppermute | solution.py:41
  51.9 11.7 %collective-permute-start.14 = (bf16[2,128,768]{2,1,0:T(8,128)(2,1)}, bf16[2,128,768]{2,1,0:T(8,128)(2,1)S(1)}, u32[]{:S(2)}, u32[]{:S(2)}) collective-permute-start(bf16[2,128,768]{2,1,0:T(8,128)(2,1)} %pad_maximum_fusion.8), channel_id=1, source_target_pairs={{0,1},{1,2},{2,3},{4,5},{5,6},{6,7},{8,9},{9,10},{10,11},{12,13},{... | collective-permute-start | bytes 1179656 | tf_op jit(solution)/shard_map/ppermute | solution.py:41
  60.2 3.5 %copy-start.6 = (f32[128,1536]{1,0:T(8,128)S(1)}, f32[128,1536]{1,0:T(8,128)}, u32[]{:S(2)}) copy-start(f32[128,1536]{1,0:T(8,128)} %get-tuple-element.32) | copy-start | bytes 2359300
  60.2 3.5 %copy-start.7 = (f32[128,1536]{1,0:T(8,128)S(1)}, f32[128,1536]{1,0:T(8,128)}, u32[]{:S(2)}) copy-start(f32[128,1536]{1,0:T(8,128)} %get-tuple-element.61) | copy-start | bytes 2359300
  61.7 2.9 %copy-start.4 = (f32[4,128,768]{2,1,0:T(8,128)S(1)}, f32[4,128,768]{2,1,0:T(8,128)}, u32[]{:S(2)}) copy-start(f32[4,128,768]{2,1,0:T(8,128)} %get-tuple-element.24) | copy-start | bytes 4718596
  61.7 2.9 %copy-start.5 = (f32[4,128,768]{2,1,0:T(8,128)S(1)}, f32[4,128,768]{2,1,0:T(8,128)}, u32[]{:S(2)}) copy-start(f32[4,128,768]{2,1,0:T(8,128)} %get-tuple-element.22) | copy-start | bytes 4718596
  61.8 12.0 %collective-permute-start.2 = (bf16[2,128,768]{2,1,0:T(8,128)(2,1)S(1)}, bf16[2,128,768]{2,1,0:T(8,128)(2,1)S(1)}, u32[]{:S(2)}, u32[]{:S(2)}) collective-permute-start(bf16[2,128,768]{2,1,0:T(8,128)(2,1)S(1)} %pad_maximum_fusion.2), channel_id=1, source_target_pairs={{3,2},{2,1},{1,0},{7,6},{6,5},{5,4},{11,10},{10,9},{9,8},{15,14},{... | collective-permute-start | bytes 1179656 | tf_op jit(solution)/shard_map/ppermute | solution.py:41
  63.9 15.2 %collective-permute-start.15 = (bf16[128,768]{1,0:T(8,128)(2,1)S(1)}, bf16[128,768]{1,0:T(8,128)(2,1)S(1)}, u32[]{:S(2)}, u32[]{:S(2)}) collective-permute-start(bf16[128,768]{1,0:T(8,128)(2,1)S(1)} %get-tuple-element.20), channel_id=1, source_target_pairs={{3,2},{7,6},{11,10},{15,14},{19,18},{23,22},{27,26},{31,30}} | collective-permute-start | bytes 589832 | tf_op jit(solution)/shard_map/ppermute | solution.py:59
  64.7 12.9 %copy-start.2 = (f32[4,128,768]{2,1,0:T(8,128)S(1)}, f32[4,128,768]{2,1,0:T(8,128)}, u32[]{:S(2)}) copy-start(f32[4,128,768]{2,1,0:T(8,128)} %get-tuple-element.23) | copy-start | bytes 4718596
  64.7 12.9 %copy-start.3 = (f32[4,128,768]{2,1,0:T(8,128)S(1)}, f32[4,128,768]{2,1,0:T(8,128)}, u32[]{:S(2)}) copy-start(f32[4,128,768]{2,1,0:T(8,128)} %get-tuple-element.21) | copy-start | bytes 4718596
  64.8 16.0 %collective-permute-start.16 = (bf16[2,128,768]{2,1,0:T(8,128)(2,1)S(1)}, bf16[2,128,768]{2,1,0:T(8,128)(2,1)S(1)}, u32[]{:S(2)}, u32[]{:S(2)}) collective-permute-start(bf16[2,128,768]{2,1,0:T(8,128)(2,1)S(1)} %pad_maximum_fusion.9), channel_id=1, source_target_pairs={{0,1},{1,2},{2,3},{4,5},{5,6},{6,7},{8,9},{9,10},{10,11},{12,13},{... | collective-permute-start | bytes 1179656 | tf_op jit(solution)/shard_map/ppermute | solution.py:41
  74.0 6.8 %collective-permute-start.3 = (bf16[128,768]{1,0:T(8,128)(2,1)S(1)}, bf16[128,768]{1,0:T(8,128)(2,1)S(1)}, u32[]{:S(2)}, u32[]{:S(2)}) collective-permute-start(bf16[128,768]{1,0:T(8,128)(2,1)S(1)} %get-tuple-element.12), channel_id=1, source_target_pairs={{0,1},{4,5},{8,9},{12,13},{16,17},{20,21},{24,25},{28,29}} | collective-permute-start | bytes 589832 | tf_op jit(solution)/shard_map/ppermute | solution.py:59
  77.8 11.4 %collective-permute-start.4 = (bf16[2,128,768]{2,1,0:T(8,128)(2,1)S(1)}, bf16[2,128,768]{2,1,0:T(8,128)(2,1)S(1)}, u32[]{:S(2)}, u32[]{:S(2)}) collective-permute-start(bf16[2,128,768]{2,1,0:T(8,128)(2,1)S(1)} %pad_maximum_fusion.3), channel_id=1, source_target_pairs={{3,2},{2,1},{1,0},{7,6},{6,5},{5,4},{11,10},{10,9},{9,8},{15,14},{... | collective-permute-start | bytes 1179656 | tf_op jit(solution)/shard_map/ppermute | solution.py:41
  79.1 10.1 %copy-start.12 = (f32[128,1536]{1,0:T(8,128)S(1)}, f32[128,1536]{1,0:T(8,128)}, u32[]{:S(2)}) copy-start(f32[128,1536]{1,0:T(8,128)} %get-tuple-element.31) | copy-start | bytes 2359300
  79.1 10.1 %copy-start.13 = (f32[128,1536]{1,0:T(8,128)S(1)}, f32[128,1536]{1,0:T(8,128)}, u32[]{:S(2)}) copy-start(f32[128,1536]{1,0:T(8,128)} %get-tuple-element.62) | copy-start | bytes 2359300
  80.9 13.4 %collective-permute-start.18 = (bf16[2,128,768]{2,1,0:T(8,128)(2,1)S(1)}, bf16[2,128,768]{2,1,0:T(8,128)(2,1)S(1)}, u32[]{:S(2)}, u32[]{:S(2)}) collective-permute-start(bf16[2,128,768]{2,1,0:T(8,128)(2,1)S(1)} %pad_maximum_fusion.10), channel_id=1, source_target_pairs={{1,2},{2,3},{5,6},{6,7},{9,10},{10,11},{13,14},{14,15},{17,18},{18... | collective-permute-start | bytes 1179656 | tf_op jit(solution)/shard_map/ppermute | solution.py:41
  89.5 4.7 %collective-permute-start.5 = (bf16[128,768]{1,0:T(8,128)(2,1)S(1)}, bf16[128,768]{1,0:T(8,128)(2,1)S(1)}, u32[]{:S(2)}, u32[]{:S(2)}) collective-permute-start(bf16[128,768]{1,0:T(8,128)(2,1)S(1)} %get-tuple-element.9), channel_id=1, source_target_pairs={{0,1},{1,2},{4,5},{5,6},{8,9},{9,10},{12,13},{13,14},{16,17},{17,1... | collective-permute-start | bytes 589832 | tf_op jit(solution)/shard_map/ppermute | solution.py:59
  91.1 3.2 %collective-permute-start.17 = (bf16[128,768]{1,0:T(8,128)(2,1)S(1)}, bf16[128,768]{1,0:T(8,128)(2,1)S(1)}, u32[]{:S(2)}, u32[]{:S(2)}) collective-permute-start(bf16[128,768]{1,0:T(8,128)(2,1)S(1)} %get-tuple-element.37), channel_id=1, source_target_pairs={{3,2},{2,1},{7,6},{6,5},{11,10},{10,9},{15,14},{14,13},{19,18},{18... | collective-permute-start | bytes 589832 | tf_op jit(solution)/shard_map/ppermute | solution.py:59
  91.9 10.5 %collective-permute-start.6 = (bf16[2,128,768]{2,1,0:T(8,128)(2,1)S(1)}, bf16[2,128,768]{2,1,0:T(8,128)(2,1)S(1)}, u32[]{:S(2)}, u32[]{:S(2)}) collective-permute-start(bf16[2,128,768]{2,1,0:T(8,128)(2,1)S(1)} %pad_maximum_fusion.4), channel_id=1, source_target_pairs={{2,1},{1,0},{6,5},{5,4},{10,9},{9,8},{14,13},{13,12},{18,17},{17,1... | collective-permute-start | bytes 1179656 | tf_op jit(solution)/shard_map/ppermute | solution.py:41
  93.3 9.2 %copy-start.10 = (f32[128,1536]{1,0:T(8,128)S(1)}, f32[128,1536]{1,0:T(8,128)}, u32[]{:S(2)}) copy-start(f32[128,1536]{1,0:T(8,128)} %get-tuple-element.30) | copy-start | bytes 2359300
  93.3 9.1 %copy-start.11 = (f32[128,1536]{1,0:T(8,128)S(1)}, f32[128,1536]{1,0:T(8,128)}, u32[]{:S(2)}) copy-start(f32[128,1536]{1,0:T(8,128)} %get-tuple-element.63) | copy-start | bytes 2359300
  94.5 23.6 %collective-permute-start.20 = (bf16[2,128,768]{2,1,0:T(8,128)(2,1)S(1)}, bf16[2,128,768]{2,1,0:T(8,128)(2,1)S(1)}, u32[]{:S(2)}, u32[]{:S(2)}) collective-permute-start(bf16[2,128,768]{2,1,0:T(8,128)(2,1)S(1)} %pad_maximum_fusion.11), channel_id=1, source_target_pairs={{2,3},{6,7},{10,11},{14,15},{18,19},{22,23},{26,27},{30,31}} | collective-permute-start | bytes 1179656 | tf_op jit(solution)/shard_map/ppermute | solution.py:41
  102.8 8.8 %collective-permute-start.7 = (bf16[128,768]{1,0:T(8,128)(2,1)S(1)}, bf16[128,768]{1,0:T(8,128)(2,1)S(1)}, u32[]{:S(2)}, u32[]{:S(2)}) collective-permute-start(bf16[128,768]{1,0:T(8,128)(2,1)S(1)} %get-tuple-element.7), channel_id=1, source_target_pairs={{0,1},{1,2},{2,3},{4,5},{5,6},{6,7},{8,9},{9,10},{10,11},{12,13},{... | collective-permute-start | bytes 589832 | tf_op jit(solution)/shard_map/ppermute | solution.py:59
  108.4 9.7 %collective-permute-start.19 = (bf16[128,768]{1,0:T(8,128)(2,1)S(1)}, bf16[128,768]{1,0:T(8,128)(2,1)S(1)}, u32[]{:S(2)}, u32[]{:S(2)}) collective-permute-start(bf16[128,768]{1,0:T(8,128)(2,1)S(1)} %get-tuple-element.35), channel_id=1, source_target_pairs={{3,2},{2,1},{1,0},{7,6},{6,5},{5,4},{11,10},{10,9},{9,8},{15,14},{... | collective-permute-start | bytes 589832 | tf_op jit(solution)/shard_map/ppermute | solution.py:59
  109.8 12.5 %copy-start.8 = (f32[128,1536]{1,0:T(8,128)S(1)}, f32[128,1536]{1,0:T(8,128)}, u32[]{:S(2)}) copy-start(f32[128,1536]{1,0:T(8,128)} %get-tuple-element.29) | copy-start | bytes 2359300
  109.8 12.5 %copy-start.9 = (f32[128,1536]{1,0:T(8,128)S(1)}, f32[128,1536]{1,0:T(8,128)}, u32[]{:S(2)}) copy-start(f32[128,1536]{1,0:T(8,128)} %get-tuple-element.64) | copy-start | bytes 2359300
  109.8 12.4 %collective-permute-start.8 = (bf16[2,128,768]{2,1,0:T(8,128)(2,1)S(1)}, bf16[2,128,768]{2,1,0:T(8,128)(2,1)S(1)}, u32[]{:S(2)}, u32[]{:S(2)}) collective-permute-start(bf16[2,128,768]{2,1,0:T(8,128)(2,1)S(1)} %pad_maximum_fusion.5), channel_id=1, source_target_pairs={{1,0},{5,4},{9,8},{13,12},{17,16},{21,20},{25,24},{29,28}} | collective-permute-start | bytes 1179656 | tf_op jit(solution)/shard_map/ppermute | solution.py:41
  122.6 4.6 %collective-permute-start.9 = (bf16[128,768]{1,0:T(8,128)(2,1)S(1)}, bf16[128,768]{1,0:T(8,128)(2,1)S(1)}, u32[]{:S(2)}, u32[]{:S(2)}) collective-permute-start(bf16[128,768]{1,0:T(8,128)(2,1)S(1)} %get-tuple-element.5), channel_id=1, source_target_pairs={{0,1},{1,2},{2,3},{4,5},{5,6},{6,7},{8,9},{9,10},{10,11},{12,13},{... | collective-permute-start | bytes 589832 | tf_op jit(solution)/shard_map/ppermute | solution.py:59
  124.1 8.5 %collective-permute-start.21 = (bf16[128,768]{1,0:T(8,128)(2,1)S(1)}, bf16[128,768]{1,0:T(8,128)(2,1)S(1)}, u32[]{:S(2)}, u32[]{:S(2)}) collective-permute-start(bf16[128,768]{1,0:T(8,128)(2,1)S(1)} %get-tuple-element.33), channel_id=1, source_target_pairs={{3,2},{2,1},{1,0},{7,6},{6,5},{5,4},{11,10},{10,9},{9,8},{15,14},{... | collective-permute-start | bytes 589832 | tf_op jit(solution)/shard_map/ppermute | solution.py:59
  127.3 6.7 %collective-permute-start.10 = (bf16[128,768]{1,0:T(8,128)(2,1)S(1)}, bf16[128,768]{1,0:T(8,128)(2,1)S(1)}, u32[]{:S(2)}, u32[]{:S(2)}) collective-permute-start(bf16[128,768]{1,0:T(8,128)(2,1)S(1)} %collective-permute-done.9), channel_id=1, source_target_pairs={{1,2},{2,3},{5,6},{6,7},{9,10},{10,11},{13,14},{14,15},{17,18},{18... | collective-permute-start | bytes 589832 | tf_op jit(solution)/shard_map/ppermute | solution.py:59
  132.6 9.6 %collective-permute-start.22 = (bf16[128,768]{1,0:T(8,128)(2,1)S(1)}, bf16[128,768]{1,0:T(8,128)(2,1)S(1)}, u32[]{:S(2)}, u32[]{:S(2)}) collective-permute-start(bf16[128,768]{1,0:T(8,128)(2,1)S(1)} %collective-permute-done.21), channel_id=1, source_target_pairs={{2,1},{1,0},{6,5},{5,4},{10,9},{9,8},{14,13},{13,12},{18,17},{17,1... | collective-permute-start | bytes 589832 | tf_op jit(solution)/shard_map/ppermute | solution.py:59
  134.0 9.6 %collective-permute-start.11 = (bf16[128,768]{1,0:T(8,128)(2,1)S(1)}, bf16[128,768]{1,0:T(8,128)(2,1)S(1)}, u32[]{:S(2)}, u32[]{:S(2)}) collective-permute-start(bf16[128,768]{1,0:T(8,128)(2,1)S(1)} %collective-permute-done.10), channel_id=1, source_target_pairs={{2,3},{6,7},{10,11},{14,15},{18,19},{22,23},{26,27},{30,31}} | collective-permute-start | bytes 589832 | tf_op jit(solution)/shard_map/ppermute | solution.py:59
  142.2 7.6 %collective-permute-start.23 = (bf16[128,768]{1,0:T(8,128)(2,1)S(1)}, bf16[128,768]{1,0:T(8,128)(2,1)S(1)}, u32[]{:S(2)}, u32[]{:S(2)}) collective-permute-start(bf16[128,768]{1,0:T(8,128)(2,1)S(1)} %collective-permute-done.22), channel_id=1, source_target_pairs={{1,0},{5,4},{9,8},{13,12},{17,16},{21,20},{25,24},{29,28}} | collective-permute-start | bytes 589832 | tf_op jit(solution)/shard_map/ppermute | solution.py:59

commit v2 on v0

v2 whole, which is shorter than its diff:
```python
import jax
import jax.numpy as jnp
from jax import lax
from jax.sharding import PartitionSpec as P

SPLIT = 2


def exchange(block, bit):
    n = lax.axis_size("tensor")
    return lax.ppermute(block, "tensor", [(i, i ^ bit) for i in range(n)])


def bits_of(n):
    return [1 << j for j in range(n.bit_length() - 1)]


def reduce_step(block, bit):
    wire = jnp.bfloat16 if lax.axis_size("tensor") <= 4 else jnp.float32
    low_side = (lax.axis_index("tensor") & bit) == 0
    half = block.shape[-1] // 2
    low, high = block[..., :half], block[..., half:]
    received = exchange(jnp.where(low_side, high, low).astype(wire), bit)
    return jnp.where(low_side, low, high) + received.astype(jnp.float32)


def gather_step(block, bit):
    low_side = (lax.axis_index("tensor") & bit) == 0
    received = exchange(block, bit)
    first = jnp.where(low_side, block, received)
    second = jnp.where(low_side, received, block)
    return jnp.concatenate([first, second], axis=-1)


def activate(block):
    return (jax.nn.silu(block[0]) * block[1]).astype(jnp.bfloat16)


def per_device(tokens, w_gate, w_up, w_down, expert_ids, route_weights):
    n_expert = lax.axis_size("expert")
    held = w_gate.shape[0]
    tok_rows, col_share = tokens.shape
    labels = jnp.arange(held * n_expert, dtype=jnp.int32)
    chosen = expert_ids[:, :, None] == labels[None, None, :]
    dense = jnp.sum(jnp.where(chosen, route_weights[:, :, None], 0.0), axis=1)
    rows_in = lax.all_gather(tokens, "expert", axis=0, tiled=True)
    dense = dense.reshape(tok_rows, n_expert, held).transpose(1, 2, 0)
    weights = lax.all_to_all(dense, "expert", split_axis=0, concat_axis=0, tiled=True)
    weights = weights.transpose(1, 0, 2).reshape(held, n_expert * tok_rows)
    pieces = []
    for e in range(held):
        for r in jnp.split(rows_in, SPLIT, axis=0):
            gate = jnp.dot(r, w_gate[e], preferred_element_type=jnp.float32)
            up = jnp.dot(r, w_up[e], preferred_element_type=jnp.float32)
            pieces.append(jnp.stack([gate, up]))
    bits = bits_of(lax.axis_size("tensor"))
    steps = [lambda x, b=b: reduce_step(x, b) for b in bits]
    steps.append(activate)
    steps += [lambda x, b=b: gather_step(x, b) for b in reversed(bits)]
    for t in range(len(steps) + len(pieces) - 1):
        for m in range(len(pieces)):
            if 0 <= t - m < len(steps):
                pieces[m] = steps[t - m](pieces[m])
    partial = 0.0
    for e in range(held):
        hidden = jnp.concatenate(pieces[e * SPLIT:(e + 1) * SPLIT], axis=0)
        result = jnp.dot(hidden, w_down[e], preferred_element_type=jnp.float32)
        partial = partial + result * weights[e][:, None]
    partial = partial.astype(jnp.bfloat16)
    partial = partial.reshape(n_expert, tok_rows, col_share)
    pieces = lax.all_to_all(partial, "expert", split_axis=0, concat_axis=0, tiled=True)
    return jnp.sum(pieces.astype(jnp.float32), axis=0).astype(jnp.bfloat16)


def solution(mesh):
    in_specs = (
        P(("group", "expert"), "tensor"),
        P("expert", "tensor", None),
        P("expert", "tensor", None),
        P("expert", None, "tensor"),
        P(("group", "expert"), None),
        P(("group", "expert"), None),
    )
    out_specs = P(("group", "expert"), "tensor")
    return jax.shard_map(
        per_device, mesh=mesh, in_specs=in_specs, out_specs=out_specs, check_vma=False
    )
```

time: 236 us -> 127 us (0.54)
  waiting for transfers between devices: 168 us -> 46.9 us
  starting transfers between devices: 3.6 us -> 25.2 us
  between operations: 13.2 us -> 0.47 us
  local copies, waits for them, and re-layouts: 9.18 us -> 1.52 us
  other arithmetic: 5.83 us -> 10.6 us
  matrix products: 17.6 us -> 20.9 us
    reduce_scatter x2 -> x0, waiting for transfers between devices: 117 us -> none  [the longest x1 62.6 us: per_device(): lax.psum_scatter(up_part, 'tensor', scatter_dimension=3, tiled=True)]
    ppermute x0 -> x16, waiting for transfers between devices: none -> 46.9 us  [exchange(): return lax.ppermute(block, 'tensor', [(i, i ^ bit) for i in range(n)])]
    all_gather x1 -> x0, waiting for transfers between devices: 36.7 us -> none  [per_device(): hidden = lax.all_gather(hidden_share, 'tensor', axis=3, tiled=True)]
    ppermute x0 -> x16, starting transfers between devices: none -> 22 us  [exchange(): return lax.ppermute(block, 'tensor', [(i, i ^ bit) for i in range(n)])]
    all_to_all x1, waiting for transfers between devices: 14.3 us -> 0.01 us  [per_device(): lax.all_to_all(dense, 'expert', split_axis=0, concat_axis=0, tiled=True)]
    all_gather x0 -> x1, blocking collectives: none -> 8.84 us  [per_device(): rows_in = lax.all_gather(tokens, 'expert', axis=0, tiled=True)]
    all_to_all x1, blocking collectives: 18.5 us -> 11.5 us  [per_device(): lax.all_to_all(partial, 'expert', split_axis=0, concat_axis=0, tiled=True)]
    add x0 -> x8, other arithmetic: none -> 5.3 us  [reduce_step(): return jnp.where(low_side, low, high) + received.astype(jnp.float32)]
  transfers between devices with their start and end apart: 4 -> 17, of which waited for: 4 -> 9; matrix products, arithmetic and copies ran while one was open for 3% -> 20% of each run, Pallas kernels for 0% -> 0%
where the time goes in v2:
time: 127 us; the launch traced here: 126 us
  waiting for transfers between devices  46.9 us (37%)
  starting transfers between devices  25.2 us (20%)
  matrix products  20.9 us (16%)
  blocking collectives  20.4 us (16%)
  other arithmetic  10.6 us (8%)
  local copies, waits for them, and re-layouts  1.52 us (1%)
    ppermute x16, waiting for transfers between devices, exchange(): return lax.ppermute(block, 'tensor', [(i, i ^ bit) for i in range(n)])  46.9 us
    ppermute x16, starting transfers between devices, exchange(): return lax.ppermute(block, 'tensor', [(i, i ^ bit) for i in range(n)])  22 us
    all_to_all x1, blocking collectives, per_device(): lax.all_to_all(partial, 'expert', split_axis=0, concat_axis=0, tiled=True)  11.5 us
    dot_general x4, matrix products, per_device(): gate = jnp.dot(r, w_gate[e], preferred_element_type=jnp.float32)  10.2 us
    all_gather x1, blocking collectives, per_device(): rows_in = lax.all_gather(tokens, 'expert', axis=0, tiled=True)  8.84 us
    dot_general x4, matrix products, per_device(): up = jnp.dot(r, w_up[e], preferred_element_type=jnp.float32)  8.7 us
    add x8, other arithmetic, reduce_step(): return jnp.where(low_side, low, high) + received.astype(jnp.float32)  5.3 us
    all_to_all x1, starting transfers between devices, per_device(): lax.all_to_all(dense, 'expert', split_axis=0, concat_axis=0, tiled=True)  3.22 us
  transfers between devices with their start and end apart: 17, of which 9 were waited for; matrix products, arithmetic and copies ran while one was open for 20% of the time, Pallas kernels for 0%

profile of v2, /device:TPU:0, one launch (start us, length us, event | category | flops | bytes accessed | tf_op | source)
XLA Modules:
  0.0 126.0 jit_solution(8113742591072346464)
XLA Ops:
  0.0 8.8 %all_gather.3 = bf16[256,1024]{1,0:T(8,128)(2,1)S(1)} all-gather(bf16[64,1024]{1,0:T(8,128)(2,1)} %param.6), channel_id=1, replica_groups=mesh['group'=2,'expert'=4,'tensor'=4] {'expert'}, dimensions={0}, use_global_device_ids=true | all-gather | bytes 655360 | tf_op jit(solution)/shard_map/all_gather | solution.py:46
  8.8 2.7 %fusion.30 = f32[1,128,1536]{2,1,0:T(8,128)S(1)} fusion(bf16[2,1024,1536]{2,1,0:T(8,128)(2,1)} %param.7, bf16[256,1024]{1,0:T(8,128)(2,1)S(1)} %all_gather.3), kind=kOutput, calls=%fused_computation.30 | convolution fusion | flops 402653184 | bytes 4194304 | tf_op jit(solution)/shard_map/dot_general | solution.py:53
  11.5 2.8 %fusion.36 = f32[1,128,1536]{2,1,0:T(8,128)S(1)} fusion(bf16[2,1024,1536]{2,1,0:T(8,128)(2,1)} %param.8, bf16[256,1024]{1,0:T(8,128)(2,1)S(1)} %all_gather.3), kind=kOutput, calls=%fused_computation.32 | convolution fusion | flops 402653184 | bytes 4194304 | tf_op jit(solution)/shard_map/dot_general | solution.py:54
  14.3 0.9 select_convert_fusion.3
  15.2 1.6 %collective-permute-start = (bf16[2,128,768]{2,1,0:T(8,128)(2,1)}, bf16[2,128,768]{2,1,0:T(8,128)(2,1)}, u32[]{:S(2)}, u32[]{:S(2)}) collective-permute-start(bf16[2,128,768]{2,1,0:T(8,128)(2,1)} %select_convert_fusion.3), channel_id=1, source_target_pairs={{0,1},{1,0},{2,3},{3,2},{4,5},{5,4},{6,7},{7,6},{8,9},{9,8},{10,11... | collective-permute-start | bytes 1179656 | tf_op jit(solution)/shard_map/ppermute | solution.py:11
  16.8 2.6 %fusion.33 = f32[1,128,1536]{2,1,0:T(8,128)S(1)} fusion(bf16[2,1024,1536]{2,1,0:T(8,128)(2,1)} %param.7, bf16[256,1024]{1,0:T(8,128)(2,1)S(1)} %all_gather.3), kind=kOutput, calls=%fused_computation.31 | convolution fusion | flops 402653184 | bytes 4194304 | tf_op jit(solution)/shard_map/dot_general | solution.py:53
  19.5 2.8 %fusion.39 = f32[1,128,1536]{2,1,0:T(8,128)S(1)} fusion(bf16[2,1024,1536]{2,1,0:T(8,128)(2,1)} %param.8, bf16[256,1024]{1,0:T(8,128)(2,1)S(1)} %all_gather.3), kind=kOutput, calls=%fused_computation.33 | convolution fusion | flops 402653184 | bytes 4194304 | tf_op jit(solution)/shard_map/dot_general | solution.py:54
  22.3 0.9 select_convert_fusion.2
  23.2 0.4 collective-permute-start.4
  23.6 2.5 %fusion.42 = f32[1,128,1536]{2,1,0:T(8,128)S(1)} fusion(bf16[2,1024,1536]{2,1,0:T(8,128)(2,1)} %param.7, bf16[256,1024]{1,0:T(8,128)(2,1)S(1)} %all_gather.3), kind=kOutput, calls=%fused_computation.34 | convolution fusion | flops 402653184 | bytes 4194304 | tf_op jit(solution)/shard_map/dot_general | solution.py:53
  26.2 0.6 fusion.48
  26.8 0.1 select_convert_fusion.1
  26.8 1.7 %collective-permute-start.8 = (bf16[2,128,768]{2,1,0:T(8,128)(2,1)S(1)}, bf16[2,128,768]{2,1,0:T(8,128)(2,1)}, u32[]{:S(2)}, u32[]{:S(2)}) collective-permute-start(bf16[2,128,768]{2,1,0:T(8,128)(2,1)S(1)} %select_convert_fusion.1), channel_id=1, source_target_pairs={{0,1},{1,0},{2,3},{3,2},{4,5},{5,4},{6,7},{7,6},{8,9},{9,8},{10,11... | collective-permute-start | bytes 1179656 | tf_op jit(solution)/shard_map/ppermute | solution.py:11
  28.5 0.7 reshape.29
  29.2 3.2 %all-to-all-start = ((f32[4,1,128]{2,1,0:T(1,128)}), f32[4,1,128]{2,1,0:T(1,128)S(1)}, u32[]{:S(2)}, u32[]{:S(2)}) async-start(f32[4,1,128]{2,1,0:T(1,128)} %reshape.29), calls=%async_computation | async-start | bytes 4096 | tf_op jit(solution)/shard_map/all_to_all | solution.py:48
  32.4 2.5 %fusion.45 = f32[1,128,1536]{2,1,0:T(8,128)S(1)} fusion(bf16[2,1024,1536]{2,1,0:T(8,128)(2,1)} %param.7, bf16[256,1024]{1,0:T(8,128)(2,1)S(1)} %all_gather.3), kind=kOutput, calls=%fused_computation.35 | convolution fusion | flops 402653184 | bytes 4194304 | tf_op jit(solution)/shard_map/dot_general | solution.py:53
  34.9 2.6 %fusion.51 = f32[1,128,1536]{2,1,0:T(8,128)S(1)} fusion(bf16[2,1024,1536]{2,1,0:T(8,128)(2,1)} %param.8, bf16[256,1024]{1,0:T(8,128)(2,1)} %copy-done.6), kind=kOutput, calls=%fused_computation.37 | convolution fusion | flops 402653184 | bytes 4194304 | tf_op jit(solution)/shard_map/dot_general | solution.py:54
  37.5 0.8 select_convert_fusion
  38.3 0.4 collective-permute-start.12
  38.8 0.5 broadcast.13
  39.3 0.7 reduce.9
  39.9 0.1 reshape.30
  40.1 0.1 mul.56
  40.1 0.1 mul.49
  40.2 1.7 %convert_add_fusion.3 = f32[2,128,768]{2,1,0:T(8,128)S(1)} fusion(bf16[2,128,768]{2,1,0:T(8,128)(2,1)} %collective-permute-done, pred[]{:T(512)S(6)} %eq.10, f32[1,128,1536]{2,1,0:T(8,128)} %copy-done.5, f32[1,128,1536]{2,1,0:T(8,128)} %copy-done.4), kind=kLoop, calls=%fused_computation.78 | loop fusion | flops 983040 | bytes 2752513 | tf_op jit(solution)/shard_map/add | solution.py:24
  42.0 2.7 %collective-permute-start.1 = (bf16[2,128,384]{2,1,0:T(8,128)(2,1)S(1)}, bf16[2,128,384]{2,1,0:T(8,128)(2,1)S(1)}, u32[]{:S(2)}, u32[]{:S(2)}) collective-permute-start(bf16[2,128,384]{2,1,0:T(8,128)(2,1)S(1)} %select_convert_fusion.7), channel_id=1, source_target_pairs={{0,2},{1,3},{2,0},{3,1},{4,6},{5,7},{6,4},{7,5},{8,10},{9,11},{10,... | collective-permute-start | bytes 589832 | tf_op jit(solution)/shard_map/ppermute | solution.py:11
  44.7 1.1 convert_add_fusion.2
  45.8 0.4 collective-permute-start.5
  46.2 1.1 convert_add_fusion.1
  47.4 2.7 %collective-permute-start.9 = (bf16[2,128,384]{2,1,0:T(8,128)(2,1)S(1)}, bf16[2,128,384]{2,1,0:T(8,128)(2,1)S(1)}, u32[]{:S(2)}, u32[]{:S(2)}) collective-permute-start(bf16[2,128,384]{2,1,0:T(8,128)(2,1)S(1)} %select_convert_fusion.5), channel_id=1, source_target_pairs={{0,2},{1,3},{2,0},{3,1},{4,6},{5,7},{6,4},{7,5},{8,10},{9,11},{10,... | collective-permute-start | bytes 589832 | tf_op jit(solution)/shard_map/ppermute | solution.py:11
  50.1 10.5 %collective-permute-done.12 = bf16[2,128,768]{2,1,0:T(8,128)(2,1)} collective-permute-done((bf16[2,128,768]{2,1,0:T(8,128)(2,1)}, bf16[2,128,768]{2,1,0:T(8,128)(2,1)}, u32[]{:S(2)}, u32[]{:S(2)}) %collective-permute-start.12) | collective-permute-done | bytes 393248 | tf_op jit(solution)/shard_map/ppermute | solution.py:11
  60.6 1.1 convert_add_fusion
  61.8 0.1 collective-permute-start.13
  62.0 0.1 fusion.91
  62.0 3.0 %collective-permute-start.2 = (bf16[128,384]{1,0:T(8,128)(2,1)S(1)}, bf16[128,384]{1,0:T(8,128)(2,1)S(1)}, u32[]{:S(2)}, u32[]{:S(2)}) collective-permute-start(bf16[128,384]{1,0:T(8,128)(2,1)S(1)} %fusion.91), channel_id=1, source_target_pairs={{0,2},{1,3},{2,0},{3,1},{4,6},{5,7},{6,4},{7,5},{8,10},{9,11},{10,... | collective-permute-start | bytes 294920 | tf_op jit(solution)/shard_map/ppermute | solution.py:11
  65.0 8.8 %collective-permute-done.5 = bf16[2,128,384]{2,1,0:T(8,128)(2,1)S(1)} collective-permute-done((bf16[2,128,384]{2,1,0:T(8,128)(2,1)S(1)}, bf16[2,128,384]{2,1,0:T(8,128)(2,1)S(1)}, u32[]{:S(2)}, u32[]{:S(2)}) %collective-permute-start.5) | collective-permute-done | bytes 196640 | tf_op jit(solution)/shard_map/ppermute | solution.py:11
  73.9 0.1 fusion.89
  74.0 0.1 collective-permute-start.6
  74.0 4.0 %collective-permute-done.9 = bf16[2,128,384]{2,1,0:T(8,128)(2,1)S(1)} collective-permute-done((bf16[2,128,384]{2,1,0:T(8,128)(2,1)S(1)}, bf16[2,128,384]{2,1,0:T(8,128)(2,1)S(1)}, u32[]{:S(2)}, u32[]{:S(2)}) %collective-permute-start.9) | collective-permute-done | bytes 196640 | tf_op jit(solution)/shard_map/ppermute | solution.py:11
  78.1 0.1 fusion.87
  78.2 0.1 collective-permute-start.10
  78.3 6.1 %collective-permute-done.13 = bf16[2,128,384]{2,1,0:T(8,128)(2,1)S(1)} collective-permute-done((bf16[2,128,384]{2,1,0:T(8,128)(2,1)S(1)}, bf16[2,128,384]{2,1,0:T(8,128)(2,1)S(1)}, u32[]{:S(2)}, u32[]{:S(2)}) %collective-permute-start.13) | collective-permute-done | bytes 196640 | tf_op jit(solution)/shard_map/ppermute | solution.py:11
  84.4 0.1 fusion.85
  84.5 0.1 collective-permute-start.14
  84.6 2.9 %collective-permute-done.2 = bf16[128,384]{1,0:T(8,128)(2,1)S(1)} collective-permute-done((bf16[128,384]{1,0:T(8,128)(2,1)S(1)}, bf16[128,384]{1,0:T(8,128)(2,1)S(1)}, u32[]{:S(2)}, u32[]{:S(2)}) %collective-permute-start.2) | collective-permute-done | bytes 98336 | tf_op jit(solution)/shard_map/ppermute | solution.py:11
  87.5 0.1 broadcast_select_fusion.15
  87.6 5.6 %collective-permute-start.3 = (bf16[128,768]{1,0:T(8,128)(2,1)S(1)}, bf16[128,768]{1,0:T(8,128)(2,1)S(1)}, u32[]{:S(2)}, u32[]{:S(2)}) collective-permute-start(bf16[128,768]{1,0:T(8,128)(2,1)S(1)} %pad_maximum_fusion.4), channel_id=1, source_target_pairs={{0,1},{1,0},{2,3},{3,2},{4,5},{5,4},{6,7},{7,6},{8,9},{9,8},{10,11... | collective-permute-start | bytes 589832 | tf_op jit(solution)/shard_map/ppermute | solution.py:11
  93.3 0.1 broadcast_select_fusion.13
  93.4 0.5 collective-permute-start.7
  93.9 0.1 broadcast_select_fusion.11
  94.1 2.0 %collective-permute-start.11 = (bf16[128,768]{1,0:T(8,128)(2,1)S(1)}, bf16[128,768]{1,0:T(8,128)(2,1)S(1)}, u32[]{:S(2)}, u32[]{:S(2)}) collective-permute-start(bf16[128,768]{1,0:T(8,128)(2,1)S(1)} %pad_maximum_fusion.6), channel_id=1, source_target_pairs={{0,1},{1,0},{2,3},{3,2},{4,5},{5,4},{6,7},{7,6},{8,9},{9,8},{10,11... | collective-permute-start | bytes 589832 | tf_op jit(solution)/shard_map/ppermute | solution.py:11
  96.0 0.3 collective-permute-done.14
  96.4 0.1 broadcast_select_fusion.9
  96.5 0.8 collective-permute-start.15
  97.3 11.0 %collective-permute-done.11 = bf16[128,768]{1,0:T(8,128)(2,1)S(1)} collective-permute-done((bf16[128,768]{1,0:T(8,128)(2,1)S(1)}, bf16[128,768]{1,0:T(8,128)(2,1)S(1)}, u32[]{:S(2)}, u32[]{:S(2)}) %collective-permute-start.11) | collective-permute-done | bytes 196640 | tf_op jit(solution)/shard_map/ppermute | solution.py:11
  108.3 0.1 broadcast_select_fusion.3
  108.4 3.1 %collective-permute-done.15 = bf16[128,768]{1,0:T(8,128)(2,1)S(1)} collective-permute-done((bf16[128,768]{1,0:T(8,128)(2,1)S(1)}, bf16[128,768]{1,0:T(8,128)(2,1)S(1)}, u32[]{:S(2)}, u32[]{:S(2)}) %collective-permute-start.15) | collective-permute-done | bytes 196640 | tf_op jit(solution)/shard_map/ppermute | solution.py:11
  111.4 0.1 broadcast_select_fusion.1
  111.5 1.0 fusion.60
  112.5 0.1 broadcast_select_fusion.7
  112.6 0.1 broadcast_select_fusion.5
  112.7 1.0 fusion.63
  113.7 11.5 %all_to_all.10 = bf16[4,64,1024]{2,1,0:T(8,128)(2,1)S(1)} all-to-all(bf16[4,64,1024]{2,1,0:T(8,128)(2,1)S(1)} %bitcast.127), channel_id=1, replica_groups=mesh['group'=2,'expert'=4,'tensor'=4] {'expert'}, dimensions={0} | all-to-all | bytes 1048576 | tf_op jit(solution)/shard_map/all_to_all | solution.py:71
  125.2 0.7 reduce_sum.22
  (51 shorter events, 0.6 us)
Async XLA Ops:
  8.8 23.6 %copy-start.6 = (bf16[256,1024]{1,0:T(8,128)(2,1)}, bf16[256,1024]{1,0:T(8,128)(2,1)S(1)}, u32[]{:S(2)}) copy-start(bf16[256,1024]{1,0:T(8,128)(2,1)S(1)} %all_gather.3) | copy-start | bytes 1572868
  11.5 3.7 %copy-start.4 = (f32[1,128,1536]{2,1,0:T(8,128)}, f32[1,128,1536]{2,1,0:T(8,128)S(1)}, u32[]{:S(2)}) copy-start(f32[1,128,1536]{2,1,0:T(8,128)S(1)} %fusion.30) | copy-start | bytes 2359300
  14.3 5.1 %copy-start.5 = (f32[1,128,1536]{2,1,0:T(8,128)}, f32[1,128,1536]{2,1,0:T(8,128)S(1)}, u32[]{:S(2)}) copy-start(f32[1,128,1536]{2,1,0:T(8,128)S(1)} %fusion.36) | copy-start | bytes 2359300
  15.2 25.0 %collective-permute-start = (bf16[2,128,768]{2,1,0:T(8,128)(2,1)}, bf16[2,128,768]{2,1,0:T(8,128)(2,1)}, u32[]{:S(2)}, u32[]{:S(2)}) collective-permute-start(bf16[2,128,768]{2,1,0:T(8,128)(2,1)} %select_convert_fusion.3), channel_id=1, source_target_pairs={{0,1},{1,0},{2,3},{3,2},{4,5},{5,4},{6,7},{7,6},{8,9},{9,8},{10,11... | collective-permute-start | bytes 1179656 | tf_op jit(solution)/shard_map/ppermute | solution.py:11
  16.8 9.3 %slice-start = ((s8[6291456]{0:T(1024)(128)(4,1)}), s8[4194304]{0:T(1024)(128)(4,1)S(1)}, s32[]{:S(2)}) async-start(s8[6291456]{0:T(1024)(128)(4,1)} %bitcast.130), calls=%async_computation.2 | async-start | bytes 8388608
  19.4 3.8 %copy-start = (f32[1,128,1536]{2,1,0:T(8,128)}, f32[1,128,1536]{2,1,0:T(8,128)S(1)}, u32[]{:S(2)}) copy-start(f32[1,128,1536]{2,1,0:T(8,128)S(1)} %fusion.33) | copy-start | bytes 2359300
  19.4 6.7 %slice-start.1 = ((s8[6291456]{0:T(1024)(128)(4,1)}), s8[2097152]{0:T(1024)(128)(4,1)S(1)}, s32[]{:S(2)}) async-start(s8[6291456]{0:T(1024)(128)(4,1)} %bitcast.130), calls=%async_computation.3 | async-start | bytes 4194304
  22.3 3.9 %copy-start.2 = (f32[1,128,1536]{2,1,0:T(8,128)}, f32[1,128,1536]{2,1,0:T(8,128)S(1)}, u32[]{:S(2)}) copy-start(f32[1,128,1536]{2,1,0:T(8,128)S(1)} %fusion.39) | copy-start | bytes 2359300
  23.2 21.5 %collective-permute-start.4 = (bf16[2,128,768]{2,1,0:T(8,128)(2,1)}, bf16[2,128,768]{2,1,0:T(8,128)(2,1)}, u32[]{:S(2)}, u32[]{:S(2)}) collective-permute-start(bf16[2,128,768]{2,1,0:T(8,128)(2,1)} %select_convert_fusion.2), channel_id=1, source_target_pairs={{0,1},{1,0},{2,3},{3,2},{4,5},{5,4},{6,7},{7,6},{8,9},{9,8},{10,11... | collective-permute-start | bytes 1179656 | tf_op jit(solution)/shard_map/ppermute | solution.py:11
  26.2 2.4 %copy-start.7 = (f32[64,8]{0,1:T(8,128)S(1)}, f32[64,8]{0,1:T(8,128)}, u32[]{:S(2)}) copy-start(f32[64,8]{0,1:T(8,128)} %param.11) | copy-start | bytes 6148
  26.2 2.3 %copy-start.8 = (s32[64,8]{0,1:T(8,128)S(1)}, s32[64,8]{0,1:T(8,128)}, u32[]{:S(2)}) copy-start(s32[64,8]{0,1:T(8,128)} %param.10) | copy-start | bytes 6148
  26.8 19.4 %collective-permute-start.8 = (bf16[2,128,768]{2,1,0:T(8,128)(2,1)S(1)}, bf16[2,128,768]{2,1,0:T(8,128)(2,1)}, u32[]{:S(2)}, u32[]{:S(2)}) collective-permute-start(bf16[2,128,768]{2,1,0:T(8,128)(2,1)S(1)} %select_convert_fusion.1), channel_id=1, source_target_pairs={{0,1},{1,0},{2,3},{3,2},{4,5},{5,4},{6,7},{7,6},{8,9},{9,8},{10,11... | collective-permute-start | bytes 1179656 | tf_op jit(solution)/shard_map/ppermute | solution.py:11
  29.2 9.6 %all-to-all-start = ((f32[4,1,128]{2,1,0:T(1,128)}), f32[4,1,128]{2,1,0:T(1,128)S(1)}, u32[]{:S(2)}, u32[]{:S(2)}) async-start(f32[4,1,128]{2,1,0:T(1,128)} %reshape.29), calls=%async_computation | async-start | bytes 4096 | tf_op jit(solution)/shard_map/all_to_all | solution.py:48
  38.3 22.3 %collective-permute-start.12 = (bf16[2,128,768]{2,1,0:T(8,128)(2,1)}, bf16[2,128,768]{2,1,0:T(8,128)(2,1)}, u32[]{:S(2)}, u32[]{:S(2)}) collective-permute-start(bf16[2,128,768]{2,1,0:T(8,128)(2,1)} %select_convert_fusion), channel_id=1, source_target_pairs={{0,1},{1,0},{2,3},{3,2},{4,5},{5,4},{6,7},{7,6},{8,9},{9,8},{10,11... | collective-permute-start | bytes 1179656 | tf_op jit(solution)/shard_map/ppermute | solution.py:11
  40.2 4.4 %copy-start.1 = (f32[1,128,1536]{2,1,0:T(8,128)S(1)}, f32[1,128,1536]{2,1,0:T(8,128)}, u32[]{:S(2)}) copy-start(f32[1,128,1536]{2,1,0:T(8,128)} %copy-done) | copy-start | bytes 2359300
  40.2 4.4 %copy-start.3 = (f32[1,128,1536]{2,1,0:T(8,128)S(1)}, f32[1,128,1536]{2,1,0:T(8,128)}, u32[]{:S(2)}) copy-start(f32[1,128,1536]{2,1,0:T(8,128)} %copy-done.2) | copy-start | bytes 2359300
  42.0 19.9 %collective-permute-start.1 = (bf16[2,128,384]{2,1,0:T(8,128)(2,1)S(1)}, bf16[2,128,384]{2,1,0:T(8,128)(2,1)S(1)}, u32[]{:S(2)}, u32[]{:S(2)}) collective-permute-start(bf16[2,128,384]{2,1,0:T(8,128)(2,1)S(1)} %select_convert_fusion.7), channel_id=1, source_target_pairs={{0,2},{1,3},{2,0},{3,1},{4,6},{5,7},{6,4},{7,5},{8,10},{9,11},{10,... | collective-permute-start | bytes 589832 | tf_op jit(solution)/shard_map/ppermute | solution.py:11
  45.8 28.0 %collective-permute-start.5 = (bf16[2,128,384]{2,1,0:T(8,128)(2,1)S(1)}, bf16[2,128,384]{2,1,0:T(8,128)(2,1)S(1)}, u32[]{:S(2)}, u32[]{:S(2)}) collective-permute-start(bf16[2,128,384]{2,1,0:T(8,128)(2,1)S(1)} %select_convert_fusion.6), channel_id=1, source_target_pairs={{0,2},{1,3},{2,0},{3,1},{4,6},{5,7},{6,4},{7,5},{8,10},{9,11},{10,... | collective-permute-start | bytes 589832 | tf_op jit(solution)/shard_map/ppermute | solution.py:11
  47.4 30.6 %collective-permute-start.9 = (bf16[2,128,384]{2,1,0:T(8,128)(2,1)S(1)}, bf16[2,128,384]{2,1,0:T(8,128)(2,1)S(1)}, u32[]{:S(2)}, u32[]{:S(2)}) collective-permute-start(bf16[2,128,384]{2,1,0:T(8,128)(2,1)S(1)} %select_convert_fusion.5), channel_id=1, source_target_pairs={{0,2},{1,3},{2,0},{3,1},{4,6},{5,7},{6,4},{7,5},{8,10},{9,11},{10,... | collective-permute-start | bytes 589832 | tf_op jit(solution)/shard_map/ppermute | solution.py:11
  61.8 22.6 %collective-permute-start.13 = (bf16[2,128,384]{2,1,0:T(8,128)(2,1)S(1)}, bf16[2,128,384]{2,1,0:T(8,128)(2,1)S(1)}, u32[]{:S(2)}, u32[]{:S(2)}) collective-permute-start(bf16[2,128,384]{2,1,0:T(8,128)(2,1)S(1)} %select_convert_fusion.4), channel_id=1, source_target_pairs={{0,2},{1,3},{2,0},{3,1},{4,6},{5,7},{6,4},{7,5},{8,10},{9,11},{10,... | collective-permute-start | bytes 589832 | tf_op jit(solution)/shard_map/ppermute | solution.py:11
  61.9 49.6 %slice-start.2 = ((s8[6291456]{0:T(1024)(128)(4,1)}), s8[4194304]{0:T(1024)(128)(4,1)S(1)}, s32[]{:S(2)}) async-start(s8[6291456]{0:T(1024)(128)(4,1)} %bitcast.132), calls=%async_computation.4 | async-start | bytes 8388608
  62.0 25.5 %collective-permute-start.2 = (bf16[128,384]{1,0:T(8,128)(2,1)S(1)}, bf16[128,384]{1,0:T(8,128)(2,1)S(1)}, u32[]{:S(2)}, u32[]{:S(2)}) collective-permute-start(bf16[128,384]{1,0:T(8,128)(2,1)S(1)} %fusion.91), channel_id=1, source_target_pairs={{0,2},{1,3},{2,0},{3,1},{4,6},{5,7},{6,4},{7,5},{8,10},{9,11},{10,... | collective-permute-start | bytes 294920 | tf_op jit(solution)/shard_map/ppermute | solution.py:11
  74.0 19.3 %collective-permute-start.6 = (bf16[128,384]{1,0:T(8,128)(2,1)S(1)}, bf16[128,384]{1,0:T(8,128)(2,1)S(1)}, u32[]{:S(2)}, u32[]{:S(2)}) collective-permute-start(bf16[128,384]{1,0:T(8,128)(2,1)S(1)} %fusion.89), channel_id=1, source_target_pairs={{0,2},{1,3},{2,0},{3,1},{4,6},{5,7},{6,4},{7,5},{8,10},{9,11},{10,... | collective-permute-start | bytes 294920 | tf_op jit(solution)/shard_map/ppermute | solution.py:11
  78.2 33.4 %slice-start.3 = ((s8[6291456]{0:T(1024)(128)(4,1)}), s8[2097152]{0:T(1024)(128)(4,1)S(1)}, s32[]{:S(2)}) async-start(s8[6291456]{0:T(1024)(128)(4,1)} %bitcast.132), calls=%async_computation.5 | async-start | bytes 4194304
  78.2 15.8 %collective-permute-start.10 = (bf16[128,384]{1,0:T(8,128)(2,1)S(1)}, bf16[128,384]{1,0:T(8,128)(2,1)S(1)}, u32[]{:S(2)}, u32[]{:S(2)}) collective-permute-start(bf16[128,384]{1,0:T(8,128)(2,1)S(1)} %fusion.87), channel_id=1, source_target_pairs={{0,2},{1,3},{2,0},{3,1},{4,6},{5,7},{6,4},{7,5},{8,10},{9,11},{10,... | collective-permute-start | bytes 294920 | tf_op jit(solution)/shard_map/ppermute | solution.py:11
  84.5 11.9 %collective-permute-start.14 = (bf16[128,384]{1,0:T(8,128)(2,1)S(1)}, bf16[128,384]{1,0:T(8,128)(2,1)S(1)}, u32[]{:S(2)}, u32[]{:S(2)}) collective-permute-start(bf16[128,384]{1,0:T(8,128)(2,1)S(1)} %fusion.85), channel_id=1, source_target_pairs={{0,2},{1,3},{2,0},{3,1},{4,6},{5,7},{6,4},{7,5},{8,10},{9,11},{10,... | collective-permute-start | bytes 294920 | tf_op jit(solution)/shard_map/ppermute | solution.py:11
  87.6 24.9 %collective-permute-start.3 = (bf16[128,768]{1,0:T(8,128)(2,1)S(1)}, bf16[128,768]{1,0:T(8,128)(2,1)S(1)}, u32[]{:S(2)}, u32[]{:S(2)}) collective-permute-start(bf16[128,768]{1,0:T(8,128)(2,1)S(1)} %pad_maximum_fusion.4), channel_id=1, source_target_pairs={{0,1},{1,0},{2,3},{3,2},{4,5},{5,4},{6,7},{7,6},{8,9},{9,8},{10,11... | collective-permute-start | bytes 589832 | tf_op jit(solution)/shard_map/ppermute | solution.py:11
  93.4 19.2 %collective-permute-start.7 = (bf16[128,768]{1,0:T(8,128)(2,1)S(1)}, bf16[128,768]{1,0:T(8,128)(2,1)S(1)}, u32[]{:S(2)}, u32[]{:S(2)}) collective-permute-start(bf16[128,768]{1,0:T(8,128)(2,1)S(1)} %pad_maximum_fusion.5), channel_id=1, source_target_pairs={{0,1},{1,0},{2,3},{3,2},{4,5},{5,4},{6,7},{7,6},{8,9},{9,8},{10,11... | collective-permute-start | bytes 589832 | tf_op jit(solution)/shard_map/ppermute | solution.py:11
  94.1 14.3 %collective-permute-start.11 = (bf16[128,768]{1,0:T(8,128)(2,1)S(1)}, bf16[128,768]{1,0:T(8,128)(2,1)S(1)}, u32[]{:S(2)}, u32[]{:S(2)}) collective-permute-start(bf16[128,768]{1,0:T(8,128)(2,1)S(1)} %pad_maximum_fusion.6), channel_id=1, source_target_pairs={{0,1},{1,0},{2,3},{3,2},{4,5},{5,4},{6,7},{7,6},{8,9},{9,8},{10,11... | collective-permute-start | bytes 589832 | tf_op jit(solution)/shard_map/ppermute | solution.py:11
  96.5 15.0 %collective-permute-start.15 = (bf16[128,768]{1,0:T(8,128)(2,1)S(1)}, bf16[128,768]{1,0:T(8,128)(2,1)S(1)}, u32[]{:S(2)}, u32[]{:S(2)}) collective-permute-start(bf16[128,768]{1,0:T(8,128)(2,1)S(1)} %pad_maximum_fusion.7), channel_id=1, source_target_pairs={{0,1},{1,0},{2,3},{3,2},{4,5},{5,4},{6,7},{7,6},{8,9},{9,8},{10,11... | collective-permute-start | bytes 589832 | tf_op jit(solution)/shard_map/ppermute | solution.py:11

commit v3 on v2

--- a/solution.py
+++ b/solution.py
@@ -3,7 +3,7 @@
 from jax import lax
 from jax.sharding import PartitionSpec as P
 
-SPLIT = 2
+NEAR = 2
 
 
 def exchange(block, bit):
@@ -36,6 +36,11 @@
     return (jax.nn.silu(block[0]) * block[1]).astype(jnp.bfloat16)
 
 
+def meet(block, offset):
+    n = lax.axis_size("expert")
+    return lax.ppermute(block, "expert", [(i, i ^ offset) for i in range(n)])
+
+
 def per_device(tokens, w_gate, w_up, w_down, expert_ids, route_weights):
     n_expert = lax.axis_size("expert")
     held = w_gate.shape[0]
@@ -43,33 +48,42 @@
     labels = jnp.arange(held * n_expert, dtype=jnp.int32)
     chosen = expert_ids[:, :, None] == labels[None, None, :]
     dense = jnp.sum(jnp.where(chosen, route_weights[:, :, None], 0.0), axis=1)
-    rows_in = lax.all_gather(tokens, "expert", axis=0, tiled=True)
-    dense = dense.reshape(tok_rows, n_expert, held).transpose(1, 2, 0)
-    weights = lax.all_to_all(dense, "expert", split_axis=0, concat_axis=0, tiled=True)
-    weights = weights.transpose(1, 0, 2).reshape(held, n_expert * tok_rows)
-    pieces = []
-    for e in range(held):
-        for r in jnp.split(rows_in, SPLIT, axis=0):
-            gate = jnp.dot(r, w_gate[e], preferred_element_type=jnp.float32)
-            up = jnp.dot(r, w_up[e], preferred_element_type=jnp.float32)
-            pieces.append(jnp.stack([gate, up]))
+    blocks = [tokens] + [meet(tokens, d) for d in range(1, n_expert)]
+    groups = [range(0, NEAR), range(NEAR, n_expert)]
+    here = lax.axis_index("expert")
     bits = bits_of(lax.axis_size("tensor"))
     steps = [lambda x, b=b: reduce_step(x, b) for b in bits]
     steps.append(activate)
     steps += [lambda x, b=b: gather_step(x, b) for b in reversed(bits)]
+    pieces = []
+    for j, group in enumerate(groups):
+        rows_in = jnp.concatenate([blocks[d] for d in group], axis=0)
+        if j == 1:
+            pieces[0] = steps[0](pieces[0])
+            pieces[0], rows_in, dense = lax.optimization_barrier((pieces[0], rows_in, dense))
+        for e in range(held):
+            gate = jnp.dot(rows_in, w_gate[e], preferred_element_type=jnp.float32)
+            up = jnp.dot(rows_in, w_up[e], preferred_element_type=jnp.float32)
+            pieces.append(jnp.stack([gate, up]))
+    dense = dense.reshape(tok_rows, n_expert, held).transpose(1, 2, 0)
+    weights = lax.all_to_all(dense, "expert", split_axis=0, concat_axis=0, tiled=True)
     for t in range(len(steps) + len(pieces) - 1):
         for m in range(len(pieces)):
-            if 0 <= t - m < len(steps):
+            if 0 <= t - m < len(steps) and t > 0:
                 pieces[m] = steps[t - m](pieces[m])
-    partial = 0.0
-    for e in range(held):
-        hidden = jnp.concatenate(pieces[e * SPLIT:(e + 1) * SPLIT], axis=0)
-        result = jnp.dot(hidden, w_down[e], preferred_element_type=jnp.float32)
-        partial = partial + result * weights[e][:, None]
-    partial = partial.astype(jnp.bfloat16)
-    partial = partial.reshape(n_expert, tok_rows, col_share)
-    pieces = lax.all_to_all(partial, "expert", split_axis=0, concat_axis=0, tiled=True)
-    return jnp.sum(pieces.astype(jnp.float32), axis=0).astype(jnp.bfloat16)
+    mixed = 0.0
+    for j, group in enumerate(groups):
+        partial = 0.0
+        rows_of = jnp.concatenate([lax.dynamic_index_in_dim(weights, here ^ d, 0, False) for d in group], axis=1)
+        for e in range(held):
+            result = jnp.dot(pieces[j * held + e], w_down[e], preferred_element_type=jnp.float32)
+            partial = partial + result * rows_of[e][:, None]
+        for i, d in enumerate(group):
+            block = partial[i * tok_rows:(i + 1) * tok_rows].astype(jnp.bfloat16)
+            if d > 0:
+                block = meet(block, d)
+            mixed = mixed + block.astype(jnp.float32)
+    return mixed.astype(jnp.bfloat16)
 
 
 def solution(mesh):

time: 127 us -> 116 us (0.913)
  blocking collectives: 20.4 us -> 0 us
  waiting for transfers between devices: 46.9 us -> 55.3 us
  matrix products: 20.9 us -> 14.8 us
  starting transfers between devices: 25.2 us -> 30.3 us
    all_to_all x1 -> x0, blocking collectives: 11.5 us -> none  [per_device(): lax.all_to_all(partial, 'expert', split_axis=0, concat_axis=0, tiled=True)]
    all_gather x1 -> x0, blocking collectives: 8.84 us -> none  [per_device(): rows_in = lax.all_gather(tokens, 'expert', axis=0, tiled=True)]
    dot_general x10 -> x12, matrix products: 20.9 us -> 14.8 us  [the longest x4 7.29 us: per_device(): gate = jnp.dot(rows_in, w_gate[e], preferred_element_type=jnp.float32)]
    ppermute x0 -> x6, waiting for transfers between devices: none -> 5.8 us  [meet(): return lax.ppermute(block, 'expert', [(i, i ^ offset) for i in range(n)])]
    ppermute x0 -> x6, starting transfers between devices: none -> 4.2 us  [meet(): return lax.ppermute(block, 'expert', [(i, i ^ offset) for i in range(n)])]
    ppermute x16, waiting for transfers between devices: 46.9 us -> 49.5 us  [exchange(): return lax.ppermute(block, 'tensor', [(i, i ^ bit) for i in range(n)])]
  transfers between devices with their start and end apart: 17 -> 23, of which waited for: 9 -> 11; matrix products, arithmetic and copies ran while one was open for 20% -> 24% of each run, Pallas kernels for 0% -> 0%
where the time goes in v3:
time: 116 us; the launch traced here: 115 us
  waiting for transfers between devices  55.3 us (48%)
  starting transfers between devices  30.3 us (26%)
  matrix products  14.8 us (13%)
  other arithmetic  11.8 us (10%)
  local copies, waits for them, and re-layouts  2.26 us (2%)
    ppermute x16, waiting for transfers between devices, exchange(): return lax.ppermute(block, 'tensor', [(i, i ^ bit) for i in range(n)])  49.5 us
    ppermute x16, starting transfers between devices, exchange(): return lax.ppermute(block, 'tensor', [(i, i ^ bit) for i in range(n)])  22.8 us
    dot_general x4, matrix products, per_device(): gate = jnp.dot(rows_in, w_gate[e], preferred_element_type=jnp.float32)  7.29 us
    ppermute x6, waiting for transfers between devices, meet(): return lax.ppermute(block, 'expert', [(i, i ^ offset) for i in range(n)])  5.8 us
    add x8, other arithmetic, reduce_step(): return jnp.where(low_side, low, high) + received.astype(jnp.float32)  4.61 us
    dot_general x4, matrix products, per_device(): jnp.dot(pieces[j * held + e], w_down[e], preferred_element_type=jnp.float32)  4.32 us
    ppermute x6, starting transfers between devices, meet(): return lax.ppermute(block, 'expert', [(i, i ^ offset) for i in range(n)])  4.2 us
    convert_element_type x8, other arithmetic, reduce_step(): received = exchange(jnp.where(low_side, high, low).astype(wire), bit)  3.95 us
  transfers between devices with their start and end apart: 23, of which 11 were waited for; matrix products, arithmetic and copies ran while one was open for 24% of the time, Pallas kernels for 0%

profile of v3, /device:TPU:0, one launch (start us, length us, event | category | flops | bytes accessed | tf_op | source)
XLA Modules:
  0.0 114.9 jit_solution(6372941067355539428)
XLA Ops:
  0.0 0.5 collective-permute-start
  0.5 2.5 %collective-permute-start.2 = (bf16[64,1024]{1,0:T(8,128)(2,1)}, bf16[64,1024]{1,0:T(8,128)(2,1)S(1)}, u32[]{:S(2)}, u32[]{:S(2)}) collective-permute-start(bf16[64,1024]{1,0:T(8,128)(2,1)} %param.6), channel_id=1, source_target_pairs={{0,8},{4,12},{8,0},{12,4},{1,9},{5,13},{9,1},{13,5},{2,10},{6,14},... | collective-permute-start | bytes 393224 | tf_op jit(solution)/shard_map/ppermute | solution.py:41
  3.0 0.1 collective-permute-start.3
  3.1 0.7 select_reduce_fusion
  3.8 0.9 constant_dynamic-update-slice_fusion.1
  4.8 2.6 %fusion.36 = f32[1,128,1536]{2,1,0:T(8,128)S(1)} fusion(bf16[128,1024]{1,0:T(8,128)(2,1)S(1)} %constant_dynamic-update-slice_fusion, bf16[2,1024,1536]{2,1,0:T(8,128)(2,1)} %param.7), kind=kOutput, calls=%fused_computation.36 | convolution fusion | flops 402653184 | bytes 4194304 | tf_op jit(solution)/shard_map/dot_general | solution.py:65
  7.4 2.6 %fusion.48 = f32[1,128,1536]{2,1,0:T(8,128)S(1)} fusion(bf16[128,1024]{1,0:T(8,128)(2,1)S(1)} %constant_dynamic-update-slice_fusion, bf16[2,1024,1536]{2,1,0:T(8,128)(2,1)} %param.7), kind=kOutput, calls=%fused_computation.40 | convolution fusion | flops 402653184 | bytes 4194304 | tf_op jit(solution)/shard_map/dot_general | solution.py:65
  10.1 0.6 fusion.42
  10.7 0.1 select_convert_fusion.3
  10.8 1.9 %collective-permute-start.1 = (bf16[2,128,768]{2,1,0:T(8,128)(2,1)S(1)}, bf16[2,128,768]{2,1,0:T(8,128)(2,1)S(1)}, u32[]{:S(2)}, u32[]{:S(2)}) collective-permute-start(bf16[2,128,768]{2,1,0:T(8,128)(2,1)S(1)} %select_convert_fusion.3), channel_id=1, source_target_pairs={{0,1},{1,0},{2,3},{3,2},{4,5},{5,4},{6,7},{7,6},{8,9},{9,8},{10,11... | collective-permute-start | bytes 1179656 | tf_op jit(solution)/shard_map/ppermute | solution.py:11
  12.7 0.6 fusion.54
  13.3 0.3 collective-permute-start.7
  13.6 9.2 %collective-permute-done.1 = bf16[2,128,768]{2,1,0:T(8,128)(2,1)S(1)} collective-permute-done((bf16[2,128,768]{2,1,0:T(8,128)(2,1)S(1)}, bf16[2,128,768]{2,1,0:T(8,128)(2,1)S(1)}, u32[]{:S(2)}, u32[]{:S(2)}) %collective-permute-start.1) | collective-permute-done | bytes 393248 | tf_op jit(solution)/shard_map/ppermute | solution.py:11
  22.8 0.1 convert_add_fusion.3
  23.0 1.5 %fusion.39 = f32[1,128,1536]{2,1,0:T(8,128)} fusion(bf16[128,1024]{1,0:T(8,128)(2,1)S(1)} %pad_maximum_fusion.4, bf16[2,1024,1536]{2,1,0:T(8,128)(2,1)S(1)} %bitcast.163), kind=kOutput, calls=%fused_computation.37 | convolution fusion | flops 402653184 | bytes 4194304 | tf_op jit(solution)/shard_map/dot_general | solution.py:65
  24.5 1.5 %fusion.45 = f32[1,128,1536]{2,1,0:T(8,128)} fusion(bf16[128,1024]{1,0:T(8,128)(2,1)S(1)} %pad_maximum_fusion.4, bf16[2,1024,1536]{2,1,0:T(8,128)(2,1)S(1)} %copy-done.2), kind=kOutput, calls=%fused_computation.39 | convolution fusion | flops 402653184 | bytes 4194304 | tf_op jit(solution)/shard_map/dot_general | solution.py:66
  26.0 0.6 fusion.51
  26.5 0.7 select_convert_fusion.7
  27.3 2.8 %collective-permute-start.4 = (bf16[2,128,384]{2,1,0:T(8,128)(2,1)}, bf16[2,128,384]{2,1,0:T(8,128)(2,1)}, u32[]{:S(2)}, u32[]{:S(2)}) collective-permute-start(bf16[2,128,384]{2,1,0:T(8,128)(2,1)} %select_convert_fusion.7), channel_id=1, source_target_pairs={{0,2},{1,3},{2,0},{3,1},{4,6},{5,7},{6,4},{7,5},{8,10},{9,11},{10,... | collective-permute-start | bytes 589832 | tf_op jit(solution)/shard_map/ppermute | solution.py:11
  30.1 0.6 fusion.57
  30.7 2.9 %collective-permute-done.7 = bf16[2,128,768]{2,1,0:T(8,128)(2,1)S(1)} collective-permute-done((bf16[2,128,768]{2,1,0:T(8,128)(2,1)S(1)}, bf16[2,128,768]{2,1,0:T(8,128)(2,1)S(1)}, u32[]{:S(2)}, u32[]{:S(2)}) %collective-permute-start.7) | collective-permute-done | bytes 393248 | tf_op jit(solution)/shard_map/ppermute | solution.py:11
  33.6 0.1 convert_add_fusion.2
  33.8 0.7 select_convert_fusion.6
  34.5 0.4 collective-permute-start.8
  34.9 0.7 reshape.10
  35.6 3.2 %all-to-all-start = ((f32[4,1,128]{2,1,0:T(1,128)}), f32[4,1,128]{2,1,0:T(1,128)S(1)}, u32[]{:S(2)}, u32[]{:S(2)}) async-start(f32[4,1,128]{2,1,0:T(1,128)} %reshape.10), calls=%async_computation | async-start | bytes 4096 | tf_op jit(solution)/shard_map/all_to_all | solution.py:69
  38.8 2.2 %select_convert_fusion.1 = bf16[2,128,768]{2,1,0:T(8,128)(2,1)} fusion(pred[]{:T(512)S(6)} %eq.10, f32[1,128,1536]{2,1,0:T(8,128)} %fusion.45, f32[1,128,1536]{2,1,0:T(8,128)} %fusion.39), kind=kLoop, calls=%fused_computation.71 | loop fusion | flops 1769472 | bytes 1966081 | tf_op jit(solution)/shard_map/convert_element_type | solution.py:23
  41.0 1.6 %collective-permute-start.12 = (bf16[2,128,768]{2,1,0:T(8,128)(2,1)}, bf16[2,128,768]{2,1,0:T(8,128)(2,1)}, u32[]{:S(2)}, u32[]{:S(2)}) collective-permute-start(bf16[2,128,768]{2,1,0:T(8,128)(2,1)} %select_convert_fusion.1), channel_id=1, source_target_pairs={{0,1},{1,0},{2,3},{3,2},{4,5},{5,4},{6,7},{7,6},{8,9},{9,8},{10,11... | collective-permute-start | bytes 1179656 | tf_op jit(solution)/shard_map/ppermute | solution.py:11
  42.7 0.4 collective-permute-start.16
  43.2 0.5 broadcast.7
  43.7 0.7 reduce
  44.4 0.1 reshape.11
  44.5 1.1 convert_add_fusion.7
  45.7 2.5 %collective-permute-start.5 = (bf16[128,384]{1,0:T(8,128)(2,1)S(1)}, bf16[128,384]{1,0:T(8,128)(2,1)S(1)}, u32[]{:S(2)}, u32[]{:S(2)}) collective-permute-start(bf16[128,384]{1,0:T(8,128)(2,1)S(1)} %fusion.107), channel_id=1, source_target_pairs={{0,2},{1,3},{2,0},{3,1},{4,6},{5,7},{6,4},{7,5},{8,10},{9,11},{10,... | collective-permute-start | bytes 294920 | tf_op jit(solution)/shard_map/ppermute | solution.py:11
  48.2 1.0 convert_add_fusion.6
  49.3 0.5 collective-permute-start.9
  49.8 13.1 %collective-permute-done.5 = bf16[128,384]{1,0:T(8,128)(2,1)S(1)} collective-permute-done((bf16[128,384]{1,0:T(8,128)(2,1)S(1)}, bf16[128,384]{1,0:T(8,128)(2,1)S(1)}, u32[]{:S(2)}, u32[]{:S(2)}) %collective-permute-start.5) | collective-permute-done | bytes 98336 | tf_op jit(solution)/shard_map/ppermute | solution.py:11
  62.9 0.1 broadcast_select_fusion.15
  63.0 3.4 %collective-permute-start.6 = (bf16[128,768]{1,0:T(8,128)(2,1)S(1)}, bf16[128,768]{1,0:T(8,128)(2,1)S(1)}, u32[]{:S(2)}, u32[]{:S(2)}) collective-permute-start(bf16[128,768]{1,0:T(8,128)(2,1)S(1)} %pad_maximum_fusion.5), channel_id=1, source_target_pairs={{0,1},{1,0},{2,3},{3,2},{4,5},{5,4},{6,7},{7,6},{8,9},{9,8},{10,11... | collective-permute-start | bytes 589832 | tf_op jit(solution)/shard_map/ppermute | solution.py:11
  66.4 0.1 broadcast_select_fusion.13
  66.5 1.5 %collective-permute-start.10 = (bf16[128,768]{1,0:T(8,128)(2,1)S(1)}, bf16[128,768]{1,0:T(8,128)(2,1)S(1)}, u32[]{:S(2)}, u32[]{:S(2)}) collective-permute-start(bf16[128,768]{1,0:T(8,128)(2,1)S(1)} %pad_maximum_fusion.6), channel_id=1, source_target_pairs={{0,1},{1,0},{2,3},{3,2},{4,5},{5,4},{6,7},{7,6},{8,9},{9,8},{10,11... | collective-permute-start | bytes 589832 | tf_op jit(solution)/shard_map/ppermute | solution.py:11
  68.0 1.1 convert_add_fusion.1
  69.2 0.7 collective-permute-start.13
  69.9 1.1 convert_add_fusion
  71.1 2.3 %collective-permute-start.17 = (bf16[2,128,384]{2,1,0:T(8,128)(2,1)S(1)}, bf16[2,128,384]{2,1,0:T(8,128)(2,1)S(1)}, u32[]{:S(2)}, u32[]{:S(2)}) collective-permute-start(bf16[2,128,384]{2,1,0:T(8,128)(2,1)S(1)} %select_convert_fusion.4), channel_id=1, source_target_pairs={{0,2},{1,3},{2,0},{3,1},{4,6},{5,7},{6,4},{7,5},{8,10},{9,11},{10,... | collective-permute-start | bytes 589832 | tf_op jit(solution)/shard_map/ppermute | solution.py:11
  73.4 6.9 %collective-permute-done.10 = bf16[128,768]{1,0:T(8,128)(2,1)S(1)} collective-permute-done((bf16[128,768]{1,0:T(8,128)(2,1)S(1)}, bf16[128,768]{1,0:T(8,128)(2,1)S(1)}, u32[]{:S(2)}, u32[]{:S(2)}) %collective-permute-start.10) | collective-permute-done | bytes 196640 | tf_op jit(solution)/shard_map/ppermute | solution.py:11
  80.4 2.5 %fusion.66 = f32[128,1024]{1,0:T(8,128)S(1)} fusion(bf16[2,1536,1024]{2,1,0:T(8,128)(2,1)} %param.9, bf16[128,768]{1,0:T(8,128)(2,1)S(1)} %get-tuple-element.14, bf16[128,768]{1,0:T(8,128)(2,1)S(1)} %get-tuple-element.13, f32[128]{0:T(128)S(1)} %get-tuple-element.34), kind=kOutput, calls=%fused_computation.54 | convolution fusion | flops 403570688 | bytes 4063744 | tf_op jit(solution)/shard_map/dot_general | solution.py:79
  83.0 0.6 fusion.78
  83.6 0.1 collective-permute-start.11
  83.7 5.3 %collective-permute-done.17 = bf16[2,128,384]{2,1,0:T(8,128)(2,1)S(1)} collective-permute-done((bf16[2,128,384]{2,1,0:T(8,128)(2,1)S(1)}, bf16[2,128,384]{2,1,0:T(8,128)(2,1)S(1)}, u32[]{:S(2)}, u32[]{:S(2)}) %collective-permute-start.17) | collective-permute-done | bytes 196640 | tf_op jit(solution)/shard_map/ppermute | solution.py:11
  89.3 3.0 %collective-permute-start.14 = (bf16[128,384]{1,0:T(8,128)(2,1)S(1)}, bf16[128,384]{1,0:T(8,128)(2,1)S(1)}, u32[]{:S(2)}, u32[]{:S(2)}) collective-permute-start(bf16[128,384]{1,0:T(8,128)(2,1)S(1)} %fusion.103), channel_id=1, source_target_pairs={{0,2},{1,3},{2,0},{3,1},{4,6},{5,7},{6,4},{7,5},{8,10},{9,11},{10,... | collective-permute-start | bytes 294920 | tf_op jit(solution)/shard_map/ppermute | solution.py:11
  92.3 5.2 %collective-permute-done.18 = bf16[128,384]{1,0:T(8,128)(2,1)S(1)} collective-permute-done((bf16[128,384]{1,0:T(8,128)(2,1)S(1)}, bf16[128,384]{1,0:T(8,128)(2,1)S(1)}, u32[]{:S(2)}, u32[]{:S(2)}) %collective-permute-start.18) | collective-permute-done | bytes 98336 | tf_op jit(solution)/shard_map/ppermute | solution.py:11
  97.5 0.1 broadcast_select_fusion.9
  97.7 0.9 collective-permute-done.14
  98.6 0.1 broadcast_select_fusion.11
  98.7 1.2 %collective-permute-start.15 = (bf16[128,768]{1,0:T(8,128)(2,1)S(1)}, bf16[128,768]{1,0:T(8,128)(2,1)S(1)}, u32[]{:S(2)}, u32[]{:S(2)}) collective-permute-start(bf16[128,768]{1,0:T(8,128)(2,1)S(1)} %pad_maximum_fusion.7), channel_id=1, source_target_pairs={{0,1},{1,0},{2,3},{3,2},{4,5},{5,4},{6,7},{7,6},{8,9},{9,8},{10,11... | collective-permute-start | bytes 589832 | tf_op jit(solution)/shard_map/ppermute | solution.py:11
  99.9 4.6 %collective-permute-done.19 = bf16[128,768]{1,0:T(8,128)(2,1)S(1)} collective-permute-done((bf16[128,768]{1,0:T(8,128)(2,1)S(1)}, bf16[128,768]{1,0:T(8,128)(2,1)S(1)}, u32[]{:S(2)}, u32[]{:S(2)}) %collective-permute-start.19) | collective-permute-done | bytes 196640 | tf_op jit(solution)/shard_map/ppermute | solution.py:11
  104.6 0.6 fusion.69
  105.3 1.4 %collective-permute-done.15 = bf16[128,768]{1,0:T(8,128)(2,1)S(1)} collective-permute-done((bf16[128,768]{1,0:T(8,128)(2,1)S(1)}, bf16[128,768]{1,0:T(8,128)(2,1)S(1)}, u32[]{:S(2)}, u32[]{:S(2)}) %collective-permute-start.15) | collective-permute-done | bytes 196640 | tf_op jit(solution)/shard_map/ppermute | solution.py:11
  106.7 0.6 fusion.81
  107.4 1.0 collective-permute-start.20
  108.4 5.0 %collective-permute-done.20 = bf16[64,1024]{1,0:T(8,128)(2,1)S(1)} collective-permute-done((bf16[64,1024]{1,0:T(8,128)(2,1)S(1)}, bf16[64,1024]{1,0:T(8,128)(2,1)S(1)}, u32[]{:S(2)}, u32[]{:S(2)}) %collective-permute-start.20) | collective-permute-done | bytes 131104 | tf_op jit(solution)/shard_map/ppermute | solution.py:41
  113.4 0.8 collective-permute-done.21
  114.2 0.7 add_convert_fusion
  (57 shorter events, 1.3 us)
Async XLA Ops:
  0.0 4.8 %collective-permute-start = (bf16[64,1024]{1,0:T(8,128)(2,1)}, bf16[64,1024]{1,0:T(8,128)(2,1)S(1)}, u32[]{:S(2)}, u32[]{:S(2)}) collective-permute-start(bf16[64,1024]{1,0:T(8,128)(2,1)} %param.6), channel_id=1, source_target_pairs={{0,4},{4,0},{8,12},{12,8},{1,5},{5,1},{9,13},{13,9},{2,6},{6,2},{1... | collective-permute-start | bytes 393224 | tf_op jit(solution)/shard_map/ppermute | solution.py:41
  0.5 13.1 %collective-permute-start.2 = (bf16[64,1024]{1,0:T(8,128)(2,1)}, bf16[64,1024]{1,0:T(8,128)(2,1)S(1)}, u32[]{:S(2)}, u32[]{:S(2)}) collective-permute-start(bf16[64,1024]{1,0:T(8,128)(2,1)} %param.6), channel_id=1, source_target_pairs={{0,8},{4,12},{8,0},{12,4},{1,9},{5,13},{9,1},{13,5},{2,10},{6,14},... | collective-permute-start | bytes 393224 | tf_op jit(solution)/shard_map/ppermute | solution.py:41
  3.0 10.6 %collective-permute-start.3 = (bf16[64,1024]{1,0:T(8,128)(2,1)}, bf16[64,1024]{1,0:T(8,128)(2,1)S(1)}, u32[]{:S(2)}, u32[]{:S(2)}) collective-permute-start(bf16[64,1024]{1,0:T(8,128)(2,1)} %param.6), channel_id=1, source_target_pairs={{0,12},{4,8},{8,4},{12,0},{1,13},{5,9},{9,5},{13,1},{2,14},{6,10},... | collective-permute-start | bytes 393224 | tf_op jit(solution)/shard_map/ppermute | solution.py:41
  4.8 5.3 %copy-start.2 = (bf16[2,1024,1536]{2,1,0:T(8,128)(2,1)S(1)}, bf16[2,1024,1536]{2,1,0:T(8,128)(2,1)}, u32[]{:S(2)}) copy-start(bf16[2,1024,1536]{2,1,0:T(8,128)(2,1)} %param.8) | copy-start | bytes 18874372
  10.6 12.3 %slice-start = ((s8[6291456]{0:T(1024)(128)(4,1)}), s8[4194304]{0:T(1024)(128)(4,1)S(1)}, s32[]{:S(2)}) async-start(s8[6291456]{0:T(1024)(128)(4,1)} %bitcast.162), calls=%async_computation.1 | async-start | bytes 8388608
  10.8 12.2 %slice-start.1 = ((s8[6291456]{0:T(1024)(128)(4,1)}), s8[2097152]{0:T(1024)(128)(4,1)S(1)}, s32[]{:S(2)}) async-start(s8[6291456]{0:T(1024)(128)(4,1)} %bitcast.162), calls=%async_computation.2 | async-start | bytes 4194304
  10.8 12.1 %collective-permute-start.1 = (bf16[2,128,768]{2,1,0:T(8,128)(2,1)S(1)}, bf16[2,128,768]{2,1,0:T(8,128)(2,1)S(1)}, u32[]{:S(2)}, u32[]{:S(2)}) collective-permute-start(bf16[2,128,768]{2,1,0:T(8,128)(2,1)S(1)} %select_convert_fusion.3), channel_id=1, source_target_pairs={{0,1},{1,0},{2,3},{3,2},{4,5},{5,4},{6,7},{7,6},{8,9},{9,8},{10,11... | collective-permute-start | bytes 1179656 | tf_op jit(solution)/shard_map/ppermute | solution.py:11
  13.3 20.3 %collective-permute-start.7 = (bf16[2,128,768]{2,1,0:T(8,128)(2,1)S(1)}, bf16[2,128,768]{2,1,0:T(8,128)(2,1)S(1)}, u32[]{:S(2)}, u32[]{:S(2)}) collective-permute-start(bf16[2,128,768]{2,1,0:T(8,128)(2,1)S(1)} %select_convert_fusion.2), channel_id=1, source_target_pairs={{0,1},{1,0},{2,3},{3,2},{4,5},{5,4},{6,7},{7,6},{8,9},{9,8},{10,11... | collective-permute-start | bytes 1179656 | tf_op jit(solution)/shard_map/ppermute | solution.py:11
  27.3 17.3 %collective-permute-start.4 = (bf16[2,128,384]{2,1,0:T(8,128)(2,1)}, bf16[2,128,384]{2,1,0:T(8,128)(2,1)}, u32[]{:S(2)}, u32[]{:S(2)}) collective-permute-start(bf16[2,128,384]{2,1,0:T(8,128)(2,1)} %select_convert_fusion.7), channel_id=1, source_target_pairs={{0,2},{1,3},{2,0},{3,1},{4,6},{5,7},{6,4},{7,5},{8,10},{9,11},{10,... | collective-permute-start | bytes 589832 | tf_op jit(solution)/shard_map/ppermute | solution.py:11
  34.5 13.8 %collective-permute-start.8 = (bf16[2,128,384]{2,1,0:T(8,128)(2,1)}, bf16[2,128,384]{2,1,0:T(8,128)(2,1)}, u32[]{:S(2)}, u32[]{:S(2)}) collective-permute-start(bf16[2,128,384]{2,1,0:T(8,128)(2,1)} %select_convert_fusion.6), channel_id=1, source_target_pairs={{0,2},{1,3},{2,0},{3,1},{4,6},{5,7},{6,4},{7,5},{8,10},{9,11},{10,... | collective-permute-start | bytes 589832 | tf_op jit(solution)/shard_map/ppermute | solution.py:11
  35.6 7.6 %all-to-all-start = ((f32[4,1,128]{2,1,0:T(1,128)}), f32[4,1,128]{2,1,0:T(1,128)S(1)}, u32[]{:S(2)}, u32[]{:S(2)}) async-start(f32[4,1,128]{2,1,0:T(1,128)} %reshape.10), calls=%async_computation | async-start | bytes 4096 | tf_op jit(solution)/shard_map/all_to_all | solution.py:69
  41.0 27.0 %collective-permute-start.12 = (bf16[2,128,768]{2,1,0:T(8,128)(2,1)}, bf16[2,128,768]{2,1,0:T(8,128)(2,1)}, u32[]{:S(2)}, u32[]{:S(2)}) collective-permute-start(bf16[2,128,768]{2,1,0:T(8,128)(2,1)} %select_convert_fusion.1), channel_id=1, source_target_pairs={{0,1},{1,0},{2,3},{3,2},{4,5},{5,4},{6,7},{7,6},{8,9},{9,8},{10,11... | collective-permute-start | bytes 1179656 | tf_op jit(solution)/shard_map/ppermute | solution.py:11
  42.7 27.2 %collective-permute-start.16 = (bf16[2,128,768]{2,1,0:T(8,128)(2,1)S(1)}, bf16[2,128,768]{2,1,0:T(8,128)(2,1)}, u32[]{:S(2)}, u32[]{:S(2)}) collective-permute-start(bf16[2,128,768]{2,1,0:T(8,128)(2,1)S(1)} %select_convert_fusion), channel_id=1, source_target_pairs={{0,1},{1,0},{2,3},{3,2},{4,5},{5,4},{6,7},{7,6},{8,9},{9,8},{10,11... | collective-permute-start | bytes 1179656 | tf_op jit(solution)/shard_map/ppermute | solution.py:11
  44.4 23.6 %copy-start = (f32[1,128,1536]{2,1,0:T(8,128)S(1)}, f32[1,128,1536]{2,1,0:T(8,128)}, u32[]{:S(2)}) copy-start(f32[1,128,1536]{2,1,0:T(8,128)} %fusion.39) | copy-start | bytes 2359300
  44.4 23.6 %copy-start.1 = (f32[1,128,1536]{2,1,0:T(8,128)S(1)}, f32[1,128,1536]{2,1,0:T(8,128)}, u32[]{:S(2)}) copy-start(f32[1,128,1536]{2,1,0:T(8,128)} %fusion.45) | copy-start | bytes 2359300
  45.7 17.2 %collective-permute-start.5 = (bf16[128,384]{1,0:T(8,128)(2,1)S(1)}, bf16[128,384]{1,0:T(8,128)(2,1)S(1)}, u32[]{:S(2)}, u32[]{:S(2)}) collective-permute-start(bf16[128,384]{1,0:T(8,128)(2,1)S(1)} %fusion.107), channel_id=1, source_target_pairs={{0,2},{1,3},{2,0},{3,1},{4,6},{5,7},{6,4},{7,5},{8,10},{9,11},{10,... | collective-permute-start | bytes 294920 | tf_op jit(solution)/shard_map/ppermute | solution.py:11
  49.3 17.1 %collective-permute-start.9 = (bf16[128,384]{1,0:T(8,128)(2,1)S(1)}, bf16[128,384]{1,0:T(8,128)(2,1)S(1)}, u32[]{:S(2)}, u32[]{:S(2)}) collective-permute-start(bf16[128,384]{1,0:T(8,128)(2,1)S(1)} %fusion.105), channel_id=1, source_target_pairs={{0,2},{1,3},{2,0},{3,1},{4,6},{5,7},{6,4},{7,5},{8,10},{9,11},{10,... | collective-permute-start | bytes 294920 | tf_op jit(solution)/shard_map/ppermute | solution.py:11
  62.9 20.0 %slice-start.2 = ((s8[6291456]{0:T(1024)(128)(4,1)}), s8[4194304]{0:T(1024)(128)(4,1)S(1)}, s32[]{:S(2)}) async-start(s8[6291456]{0:T(1024)(128)(4,1)} %bitcast.164), calls=%async_computation.3 | async-start | bytes 8388608
  63.0 19.8 %collective-permute-start.6 = (bf16[128,768]{1,0:T(8,128)(2,1)S(1)}, bf16[128,768]{1,0:T(8,128)(2,1)S(1)}, u32[]{:S(2)}, u32[]{:S(2)}) collective-permute-start(bf16[128,768]{1,0:T(8,128)(2,1)S(1)} %pad_maximum_fusion.5), channel_id=1, source_target_pairs={{0,1},{1,0},{2,3},{3,2},{4,5},{5,4},{6,7},{7,6},{8,9},{9,8},{10,11... | collective-permute-start | bytes 589832 | tf_op jit(solution)/shard_map/ppermute | solution.py:11
  66.5 13.8 %collective-permute-start.10 = (bf16[128,768]{1,0:T(8,128)(2,1)S(1)}, bf16[128,768]{1,0:T(8,128)(2,1)S(1)}, u32[]{:S(2)}, u32[]{:S(2)}) collective-permute-start(bf16[128,768]{1,0:T(8,128)(2,1)S(1)} %pad_maximum_fusion.6), channel_id=1, source_target_pairs={{0,1},{1,0},{2,3},{3,2},{4,5},{5,4},{6,7},{7,6},{8,9},{9,8},{10,11... | collective-permute-start | bytes 589832 | tf_op jit(solution)/shard_map/ppermute | solution.py:11
  69.2 13.8 %slice-start.3 = ((s8[6291456]{0:T(1024)(128)(4,1)}), s8[2097152]{0:T(1024)(128)(4,1)S(1)}, s32[]{:S(2)}) async-start(s8[6291456]{0:T(1024)(128)(4,1)} %bitcast.164), calls=%async_computation.4 | async-start | bytes 4194304
  69.2 20.0 %collective-permute-start.13 = (bf16[2,128,384]{2,1,0:T(8,128)(2,1)S(1)}, bf16[2,128,384]{2,1,0:T(8,128)(2,1)S(1)}, u32[]{:S(2)}, u32[]{:S(2)}) collective-permute-start(bf16[2,128,384]{2,1,0:T(8,128)(2,1)S(1)} %select_convert_fusion.5), channel_id=1, source_target_pairs={{0,2},{1,3},{2,0},{3,1},{4,6},{5,7},{6,4},{7,5},{8,10},{9,11},{10,... | collective-permute-start | bytes 589832 | tf_op jit(solution)/shard_map/ppermute | solution.py:11
  71.1 17.9 %collective-permute-start.17 = (bf16[2,128,384]{2,1,0:T(8,128)(2,1)S(1)}, bf16[2,128,384]{2,1,0:T(8,128)(2,1)S(1)}, u32[]{:S(2)}, u32[]{:S(2)}) collective-permute-start(bf16[2,128,384]{2,1,0:T(8,128)(2,1)S(1)} %select_convert_fusion.4), channel_id=1, source_target_pairs={{0,2},{1,3},{2,0},{3,1},{4,6},{5,7},{6,4},{7,5},{8,10},{9,11},{10,... | collective-permute-start | bytes 589832 | tf_op jit(solution)/shard_map/ppermute | solution.py:11
  83.6 24.8 %collective-permute-start.11 = (bf16[64,1024]{1,0:T(8,128)(2,1)S(1)}, bf16[64,1024]{1,0:T(8,128)(2,1)S(1)}, u32[]{:S(2)}, u32[]{:S(2)}) collective-permute-start(bf16[64,1024]{1,0:T(8,128)(2,1)S(1)} %slice.173), channel_id=1, source_target_pairs={{0,4},{4,0},{8,12},{12,8},{1,5},{5,1},{9,13},{13,9},{2,6},{6,2},{1... | collective-permute-start | bytes 393224 | tf_op jit(solution)/shard_map/ppermute | solution.py:41
  89.1 8.4 %collective-permute-start.18 = (bf16[128,384]{1,0:T(8,128)(2,1)S(1)}, bf16[128,384]{1,0:T(8,128)(2,1)S(1)}, u32[]{:S(2)}, u32[]{:S(2)}) collective-permute-start(bf16[128,384]{1,0:T(8,128)(2,1)S(1)} %fusion.101), channel_id=1, source_target_pairs={{0,2},{1,3},{2,0},{3,1},{4,6},{5,7},{6,4},{7,5},{8,10},{9,11},{10,... | collective-permute-start | bytes 294920 | tf_op jit(solution)/shard_map/ppermute | solution.py:11
  89.3 9.3 %collective-permute-start.14 = (bf16[128,384]{1,0:T(8,128)(2,1)S(1)}, bf16[128,384]{1,0:T(8,128)(2,1)S(1)}, u32[]{:S(2)}, u32[]{:S(2)}) collective-permute-start(bf16[128,384]{1,0:T(8,128)(2,1)S(1)} %fusion.103), channel_id=1, source_target_pairs={{0,2},{1,3},{2,0},{3,1},{4,6},{5,7},{6,4},{7,5},{8,10},{9,11},{10,... | collective-permute-start | bytes 294920 | tf_op jit(solution)/shard_map/ppermute | solution.py:11
  97.7 6.9 %collective-permute-start.19 = (bf16[128,768]{1,0:T(8,128)(2,1)S(1)}, bf16[128,768]{1,0:T(8,128)(2,1)S(1)}, u32[]{:S(2)}, u32[]{:S(2)}) collective-permute-start(bf16[128,768]{1,0:T(8,128)(2,1)S(1)} %pad_maximum_fusion.8), channel_id=1, source_target_pairs={{0,1},{1,0},{2,3},{3,2},{4,5},{5,4},{6,7},{7,6},{8,9},{9,8},{10,11... | collective-permute-start | bytes 589832 | tf_op jit(solution)/shard_map/ppermute | solution.py:11
  98.7 7.9 %collective-permute-start.15 = (bf16[128,768]{1,0:T(8,128)(2,1)S(1)}, bf16[128,768]{1,0:T(8,128)(2,1)S(1)}, u32[]{:S(2)}, u32[]{:S(2)}) collective-permute-start(bf16[128,768]{1,0:T(8,128)(2,1)S(1)} %pad_maximum_fusion.7), channel_id=1, source_target_pairs={{0,1},{1,0},{2,3},{3,2},{4,5},{5,4},{6,7},{7,6},{8,9},{9,8},{10,11... | collective-permute-start | bytes 589832 | tf_op jit(solution)/shard_map/ppermute | solution.py:11
  107.4 6.0 %collective-permute-start.20 = (bf16[64,1024]{1,0:T(8,128)(2,1)S(1)}, bf16[64,1024]{1,0:T(8,128)(2,1)S(1)}, u32[]{:S(2)}, u32[]{:S(2)}) collective-permute-start(bf16[64,1024]{1,0:T(8,128)(2,1)S(1)} %get-tuple-element.19), channel_id=1, source_target_pairs={{0,8},{4,12},{8,0},{12,4},{1,9},{5,13},{9,1},{13,5},{2,10},{6,14},... | collective-permute-start | bytes 393224 | tf_op jit(solution)/shard_map/ppermute | solution.py:41
  108.4 5.8 %collective-permute-start.21 = (bf16[64,1024]{1,0:T(8,128)(2,1)S(1)}, bf16[64,1024]{1,0:T(8,128)(2,1)S(1)}, u32[]{:S(2)}, u32[]{:S(2)}) collective-permute-start(bf16[64,1024]{1,0:T(8,128)(2,1)S(1)} %get-tuple-element.20), channel_id=1, source_target_pairs={{0,12},{4,8},{8,4},{12,0},{1,13},{5,9},{9,5},{13,1},{2,14},{6,10},... | collective-permute-start | bytes 393224 | tf_op jit(solution)/shard_map/ppermute | solution.py:41
